TPU v7x, 32 devices: a whole 2x2x4 slice. The times are simulated.
32 devices in a mesh: px: 2 (over core), pz: 16 (over z, y, x).
Axes of the slice: x: 2, y: 2, z: 4, core: 2. Of those that a mesh axis runs over, the one named last changes fastest.
Arguments:
- velocity: float32 [3, 256, 32, 256], P(None, 'pz', None, 'px'), may hold values from -8 to 8, as said below
- filter_inverse: float32 [256, 256], replicated, may hold values from 0 to 2, as said below
- filter_block: int32 [256], replicated, may hold values from 0 to 7, never falling along the last dimension, each value on 1 to 128 neighbouring positions
- plane_bin: int32 [256], replicated, may hold values from 0 to 63, never falling along the last dimension, each value on 1 to 16 neighbouring positions
Outputs:
- leonard: float32 [6, 256, 32, 256], P(None, 'pz', None, 'px')
- viscosity: float32 [256, 32, 256], P('pz', None, 'px')
- coefficient: float32 [256], replicated
Inputs may be any that keep to these rules, and one draw needn't show every extreme that they name: `velocity`: each component is a rough random field. `filter_inverse`: entries are positive. `filter_block`: never falls along the planes; each of the 8 blocks holds 1 to 128 consecutive planes, one exactly 128. `plane_bin`: never falls along the planes; each of the 64 bins holds 1 to 16 consecutive planes, one exactly 16.
All inputs are finite; a program needn't handle non-finite values.
Results may differ from a plain program's by a relative error of at most 0.0003.
Values sent between devices are 32-bit elements; how exact they have to be, the bound alone decides.
A program may use at most 128 MiB of HBM per device.

v0:
```python
import jax
import jax.numpy as jnp
from jax import lax
from jax.sharding import PartitionSpec as P

NBIN = 64


def with_halo(cells, sides, width, closed):
    for axis, dim in sides:
        count = lax.axis_size(axis)
        ends = count if closed else count - 1
        head = lax.slice_in_dim(cells, 0, width, axis=dim)
        tail = lax.slice_in_dim(cells, cells.shape[dim] - width, cells.shape[dim], axis=dim)
        cells = jnp.concatenate(
            [
                lax.ppermute(tail, axis, [(i, (i + 1) % count) for i in range(ends)]),
                cells,
                lax.ppermute(head, axis, [((i + 1) % count, i) for i in range(ends)]),
            ],
            axis=dim,
        )
    return cells


def quantities(padded):
    centre = padded[:, 1:-1, 1:-1, 1:-1]
    along_y = (padded[:, 2:, 1:-1, 1:-1] - padded[:, :-2, 1:-1, 1:-1]) * 0.5
    along_z = (padded[:, 1:-1, 2:, 1:-1] - padded[:, 1:-1, :-2, 1:-1]) * 0.5
    along_x = (padded[:, 1:-1, 1:-1, 2:] - padded[:, 1:-1, 1:-1, :-2]) * 0.5
    strain = jnp.stack(
        [
            along_x[0],
            along_y[1],
            along_z[2],
            0.5 * (along_y[0] + along_x[1]),
            0.5 * (along_z[0] + along_x[2]),
            0.5 * (along_z[1] + along_y[2]),
        ]
    )
    magnitude = jnp.sqrt(
        2.0 * jnp.sum(strain[:3] * strain[:3], axis=0)
        + 4.0 * jnp.sum(strain[3:] * strain[3:], axis=0)
    )
    products = jnp.stack(
        [
            centre[0] * centre[0],
            centre[1] * centre[1],
            centre[2] * centre[2],
            centre[0] * centre[1],
            centre[0] * centre[2],
            centre[1] * centre[2],
        ]
    )
    fields = jnp.concatenate([centre, strain, products, magnitude[None] * strain], axis=0)
    along = (fields[..., :-2] + 2.0 * fields[..., 1:-1] + fields[..., 2:]) * 0.25
    boxed = (along[:, :, :-2] + 2.0 * along[:, :, 1:-1] + along[:, :, 2:]) * 0.25
    return (boxed, magnitude[:, 1:-1, 1:-1])


def contract(filtered):
    speed = filtered[0:3]
    strain = filtered[3:9]
    products = filtered[9:15]
    scaled = filtered[15:21]
    leonard = products - jnp.stack(
        [
            speed[0] * speed[0],
            speed[1] * speed[1],
            speed[2] * speed[2],
            speed[0] * speed[1],
            speed[0] * speed[2],
            speed[1] * speed[2],
        ]
    )
    fmag = jnp.sqrt(
        2.0 * jnp.sum(strain[:3] * strain[:3], axis=0)
        + 4.0 * jnp.sum(strain[3:] * strain[3:], axis=0)
    )
    model = scaled - 4.0 * fmag[None] * strain
    weights = jnp.array([1.0, 1.0, 1.0, 2.0, 2.0, 2.0], jnp.float32).reshape(6, 1, 1, 1)
    product_lm = jnp.sum(weights * leonard * model, axis=0)
    product_mm = jnp.sum(weights * model * model, axis=0)
    return (leonard, product_lm, product_mm)


def local(velocity, filter_inverse, filter_block, plane_bin):
    same = (filter_block[:, None] == filter_block[None, :]).astype(jnp.float32)
    masked = filter_inverse * same
    weights = masked / jnp.sum(masked, axis=1, keepdims=True)
    local_planes = velocity.shape[1]
    extended = with_halo(velocity, (("px", 3),), 2, True)
    extended = with_halo(extended, (("pz", 1),), 1, False)
    extended = jnp.concatenate([extended[:, :, -2:], extended, extended[:, :, :2]], axis=2)
    boxed, magnitude = quantities(extended)
    smooth_boxed = lax.all_to_all(boxed, "pz", split_axis=2, concat_axis=1, tiled=True)
    filtered = jnp.einsum("ab,kbzx->kazx", weights, smooth_boxed, precision=lax.Precision.HIGHEST)
    leonard, product_lm, product_mm = contract(filtered)
    onehot = (plane_bin[:, None] == jnp.arange(NBIN, dtype=jnp.int32)[None, :]).astype(jnp.float32)
    local_lm = jnp.dot(jnp.sum(product_lm, axis=(1, 2)), onehot, precision=lax.Precision.HIGHEST)
    local_mm = jnp.dot(jnp.sum(product_mm, axis=(1, 2)), onehot, precision=lax.Precision.HIGHEST)
    numer, denom = lax.psum((local_lm, local_mm), ("px", "pz"))
    cells = filtered.shape[3] * lax.axis_size("px") * filtered.shape[2] * lax.axis_size("pz")
    per_bin = numer / jnp.maximum(denom, jnp.float32(cells))
    coefficient = jnp.dot(onehot, per_bin, precision=lax.Precision.HIGHEST)
    leonard_back = lax.all_to_all(leonard, "pz", split_axis=1, concat_axis=2, tiled=True)
    offset = lax.axis_index("pz") * local_planes
    local_coef = lax.dynamic_slice_in_dim(coefficient, offset, local_planes, 0)
    viscosity = local_coef[:, None, None] * magnitude
    return (leonard_back, viscosity, coefficient)


def solution(mesh):
    return jax.shard_map(
        local,
        mesh=mesh,
        in_specs=(P(None, "pz", None, "px"), P(), P(), P()),
        out_specs=(P(None, "pz", None, "px"), P("pz", None, "px"), P()),
        check_vma=False,
    )
```

profile of v0, /device:TPU:31, one launch (start us, length us, event | category | flops | bytes accessed | tf_op | source)
XLA Modules:
  0.0 243.1 jit_solution(18244381259723919933)
XLA Ops:
  0.6 1.7 fusion.38
  2.7 0.7 collective-permute-start
  5.5 0.7 pad_maximum_fusion.18
  6.2 1.3 collective-permute-start.2
  7.5 4.2 %collective-permute-start.3 = (f32[3,1,32,132]{3,1,0,2:T(1,128)S(1)}, f32[3,1,32,132]{3,1,0,2:T(1,128)S(1)}, u32[]{:S(2)}, u32[]{:S(2)}) collective-permute-start(f32[3,1,32,132]{3,1,0,2:T(1,128)S(1)} %get-tuple-element.28), channel_id=1, source_target_pairs={{1,0},{2,1},{3,2},{4,3},{5,4},{6,5},{7,6},{8,7},{9,8},{10,9},{11,1... | collective-permute-start | bytes 152072 | tf_op jit(solution)/shard_map/ppermute | solution.py:19
  11.7 0.6 collective-permute-done.2
  12.2 0.9 collective-permute-done.3
  13.3 1.0 pad_maximum_fusion
  14.3 3.0 %fusion.6 = (f32[3,16,34,130]{3,1,0,2:T(8,128)}, f32[3,16,34,130]{3,1,0,2:T(8,128)S(1)}, f32[21,16,34,130]{3,1,0,2:T(8,128)S(1)}) fusion(f32[3,18,36,132]{3,1,0,2:T(8,128)S(1)} %pad_maximum_fusion), kind=kLoop, calls=%fused_computation.25 | loop fusion | flops 848639 | bytes 8434176 | tf_op jit(solution)/shard_map/mul | solution.py:28
  17.5 1.2 fusion.36
  18.7 2.1 fusion.5
  24.0 0.5 multiply_dynamic-update-slice_fusion
  24.5 3.2 %fusion = f32[21,16,34,128]{3,1,0,2:T(8,128)S(1)} fusion(f32[21,16,34,130]{3,1,0,2:T(8,128)S(1)} %multiply_dynamic-update-slice_fusion), kind=kLoop, calls=%fused_computation.1 | loop fusion | flops 5849088 | bytes 23396352 | tf_op jit(solution)/shard_map/mul | solution.py:56
  27.7 3.2 %fusion.2 = f32[21,16,32,128]{3,1,0,2:T(8,128)} fusion(f32[21,16,34,128]{3,1,0,2:T(8,128)S(1)} %fusion), kind=kLoop, calls=%fused_computation.5 | loop fusion | flops 5505024 | bytes 22020096 | tf_op jit(solution)/shard_map/mul | solution.py:57
  30.9 9.3 %all-to-all-start = ((f32[21,16,32,128]{3,1,0,2:T(8,128)}), f32[21,16,32,128]{3,1,0,2:T(8,128)}, u32[]{:S(2)}, u32[]{:S(2)}) async-start(f32[21,16,32,128]{3,1,0,2:T(8,128)} %fusion.2), calls=%async_computation | async-start | bytes 11010048 | tf_op jit(solution)/shard_map/all_to_all | solution.py:96
  40.4 118.5 %all-to-all-done = f32[21,16,32,128]{3,1,0,2:T(8,128)} async-done(((f32[21,16,32,128]{3,1,0,2:T(8,128)}), f32[21,16,32,128]{3,1,0,2:T(8,128)}, u32[]{:S(2)}, u32[]{:S(2)}) %all-to-all-start) | async-done | bytes 5505056 | tf_op jit(solution)/shard_map/all_to_all | solution.py:96
  158.9 3.3 %copy.29 = f32[21,16,16,2,128]{4,2,1,3,0:T(8,128)S(1)} copy(f32[21,16,16,2,128]{4,2,0,3,1:T(8,128)} %bitcast.2) | data formatting | bytes 11010048 | tf_op jit(solution)/shard_map/all_to_all | solution.py:96
  162.2 8.8 %convolution_bitcast_fusion = f32[21,256,2,128]{1,3,2,0:T(8,128)S(1)} fusion(f32[21,256,2,128]{3,1,2,0:T(8,128)S(1)} %bitcast.28, f32[256,256]{1,0:T(8,128)S(1)} %copy-done.2, f32[256]{0:T(256)S(1)} %fusion.19, s32[256]{0:T(256)S(1)} %copy-done.3), kind=kOutput, calls=%fused_computation.10 | convolution fusion | flops 4228055040 | bytes 11274240 | tf_op jit(solution)/shard_map/ab,kbzx->kazx/dot_general | solution.py:97
  171.8 0.7 fusion.10
  172.6 2.1 copy.31
  174.6 9.0 %all-to-all-start.1 = ((f32[6,256,2,128]{3,2,0,1:T(2,128)}), f32[6,256,2,128]{3,2,0,1:T(2,128)S(1)}, u32[]{:S(2)}, u32[]{:S(2)}) async-start(f32[6,256,2,128]{3,2,0,1:T(2,128)} %copy.31), calls=%async_computation.1 | async-start | bytes 3145728 | tf_op jit(solution)/shard_map/all_to_all | solution.py:106
  184.1 55.8 %all-reduce = (f32[64]{0:T(128)S(1)}, f32[64]{0:T(128)S(1)}) all-reduce(f32[64]{0:T(128)S(1)} %convolution_bitcast_fusion.2, f32[64]{0:T(128)S(1)} %convolution_bitcast_fusion.1), channel_id=1, replica_groups=mesh['px'=2,'pz'=16] {'px','pz'}, use_global_device_ids=true, to_apply=%region_6.0 | all-reduce | flops 128 | bytes 1024 | tf_op jit(solution)/shard_map/psum | solution.py:102
  240.4 0.8 copy.35
  241.5 1.6 copy.34
  (56 shorter events, 8.0 us)
Async XLA Ops:
  0.6 3.2 %copy-start = (f32[3,16,32,128]{3,2,1,0:T(8,128)S(1)}, f32[3,16,32,128]{3,2,1,0:T(8,128)}, u32[]{:S(2)}) copy-start(f32[3,16,32,128]{3,2,1,0:T(8,128)} %param.5) | copy-start | bytes 2359300
  2.7 1.6 collective-permute-start
  3.8 1.3 collective-permute-start.1
  6.2 6.1 %collective-permute-start.2 = (f32[3,1,32,132]{3,1,0,2:T(1,128)S(1)}, f32[3,1,32,132]{3,1,0,2:T(1,128)S(1)}, u32[]{:S(2)}, u32[]{:S(2)}) collective-permute-start(f32[3,1,32,132]{3,1,0,2:T(1,128)S(1)} %get-tuple-element.27), channel_id=1, source_target_pairs={{0,1},{1,2},{2,3},{3,4},{4,5},{5,6},{6,7},{7,8},{8,9},{9,10},{10,1... | collective-permute-start | bytes 152072 | tf_op jit(solution)/shard_map/ppermute | solution.py:17
  7.5 5.6 %collective-permute-start.3 = (f32[3,1,32,132]{3,1,0,2:T(1,128)S(1)}, f32[3,1,32,132]{3,1,0,2:T(1,128)S(1)}, u32[]{:S(2)}, u32[]{:S(2)}) collective-permute-start(f32[3,1,32,132]{3,1,0,2:T(1,128)S(1)} %get-tuple-element.28), channel_id=1, source_target_pairs={{1,0},{2,1},{3,2},{4,3},{5,4},{6,5},{7,6},{8,7},{9,8},{10,9},{11,1... | collective-permute-start | bytes 152072 | tf_op jit(solution)/shard_map/ppermute | solution.py:19
  18.7 2.3 copy-start.1
  30.9 9.3 %copy-start.2 = (f32[256,256]{1,0:T(8,128)S(1)}, f32[256,256]{1,0:T(8,128)}, u32[]{:S(2)}) copy-start(f32[256,256]{1,0:T(8,128)} %param.6) | copy-start | bytes 786436
  30.9 9.3 %copy-start.3 = (s32[256]{0:T(256)S(1)}, s32[256]{0:T(256)}, u32[]{:S(2)}) copy-start(s32[256]{0:T(256)} %param.7) | copy-start | bytes 3076
  30.9 128.0 %all-to-all-start = ((f32[21,16,32,128]{3,1,0,2:T(8,128)}), f32[21,16,32,128]{3,1,0,2:T(8,128)}, u32[]{:S(2)}, u32[]{:S(2)}) async-start(f32[21,16,32,128]{3,1,0,2:T(8,128)} %fusion.2), calls=%async_computation | async-start | bytes 11010048 | tf_op jit(solution)/shard_map/all_to_all | solution.py:96
  171.1 0.7 copy-start.4
  172.5 11.1 %copy-start.5 = (s32[256]{0:T(256)S(1)}, s32[256]{0:T(256)}, u32[]{:S(2)}) copy-start(s32[256]{0:T(256)} %param.8) | copy-start | bytes 3076
  174.6 66.5 %all-to-all-start.1 = ((f32[6,256,2,128]{3,2,0,1:T(2,128)}), f32[6,256,2,128]{3,2,0,1:T(2,128)S(1)}, u32[]{:S(2)}, u32[]{:S(2)}) async-start(f32[6,256,2,128]{3,2,0,1:T(2,128)} %copy.31), calls=%async_computation.1 | async-start | bytes 3145728 | tf_op jit(solution)/shard_map/all_to_all | solution.py:106
  240.1 1.4 copy-start.6
where the time goes:
time: 247 us; the launch traced here: 243 us
  waiting for transfers between devices  120 us (49%)
  blocking collectives  55.8 us (23%)
  starting transfers between devices  24.5 us (10%)
  other arithmetic  18.2 us (7%)
  local copies, waits for them, and re-layouts  14 us (6%)
  matrix products  9.46 us (4%)
    all_to_all x1, waiting for transfers between devices, local(): lax.all_to_all(boxed, 'pz', split_axis=2, concat_axis=1, tiled=True)  119 us
    psum x1, blocking collectives, local(): numer, denom = lax.psum((local_lm, local_mm), ('px', 'pz'))  55.8 us
    all_to_all x1, starting transfers between devices, local(): lax.all_to_all(boxed, 'pz', split_axis=2, concat_axis=1, tiled=True)  9.26 us
    all_to_all x1, starting transfers between devices, local(): lax.all_to_all(leonard, 'pz', split_axis=1, concat_axis=2, tiled=True)  8.97 us
    dot_general x1, matrix products, local(): jnp.einsum('ab,kbzx->kazx', weights, smooth_boxed, precision=lax.Precisio...  8.81 us
  transfers between devices with their start and end apart: 6, of which 4 were waited for; matrix products, arithmetic and copies ran while one was open for 1% of the time, Pallas kernels for 0%

commit v1 on v0

v1 whole, which is shorter than its diff:
```python
import functools

import jax
import jax.numpy as jnp
from jax import lax
from jax.experimental import pallas as pl
from jax.experimental.pallas import tpu as pltpu
from jax.sharding import PartitionSpec as P

NBIN = 64
PAIRS = ((0, 0), (1, 1), (2, 2), (0, 1), (0, 2), (1, 2))


def tensor_norm(s):
    diag = s[0] * s[0] + s[1] * s[1] + s[2] * s[2]
    off = s[3] * s[3] + s[4] * s[4] + s[5] * s[5]
    return jnp.sqrt(2.0 * diag + 4.0 * off)


def column_kernel(dims, own, right, left, weights, onehot_t, back, sums, ext, bhi, blo, filt, lms, mms, whi, wlo):
    n, win, lp, nx = dims
    zs = win - 4
    ny = n * lp
    lanes = 2 * nx
    lane = lax.broadcasted_iota(jnp.int32, (lp, nx), 1)
    from_right = lane < nx // 2

    heavy = weights[...].astype(jnp.bfloat16)
    whi[...] = heavy
    wlo[...] = (weights[...] - heavy.astype(jnp.float32)).astype(jnp.bfloat16)

    zero = jnp.zeros((8, lanes), jnp.float32)
    for c in range(3):
        for z in range(win):
            ext[c, z, 0:8, :] = zero
            ext[c, z, ny + 8 : ny + 16, :] = zero

    @pl.loop(0, n)
    def _(p):
        rows = pl.ds(pl.multiple_of(8 + p * lp, 8), lp)
        for c in range(3):
            for z in range(win):
                ext[c, z, rows, 0:nx] = own[p, c, z]
                ext[c, z, rows, nx:lanes] = jnp.where(from_right, right[p, c, z], left[p, c, z])

    @pl.loop(0, n)
    def _(p):
        base = pl.multiple_of(p * lp, 8)
        u = [[ext[c, z, pl.ds(base + 8, lp), :] for z in range(win)] for c in range(3)]
        boxes = [[None] * 21 for _ in range(zs)]
        for z in range(1, win - 1):
            v = [u[c][z] for c in range(3)]
            dx, dy, dz = [], [], []
            for c in range(3):
                dx.append(pltpu.roll(v[c], lanes - 1, 1) - pltpu.roll(v[c], 1, 1))
                tall = ext[c, z, pl.ds(base, lp + 16), :]
                dy.append(tall[9 : 9 + lp] - tall[7 : 7 + lp])
                dz.append(u[c][z + 1] - u[c][z - 1])
            s = [
                dx[0] * 0.5,
                dy[1] * 0.5,
                dz[2] * 0.5,
                0.25 * (dy[0] + dx[1]),
                0.25 * (dz[0] + dx[2]),
                0.25 * (dz[1] + dy[2]),
            ]
            mag = tensor_norm(s)
            fields = v + s + [v[i] * v[j] for i, j in PAIRS] + [mag * t for t in s]
            if 2 <= z < win - 2:
                back[p, 6, z - 2] = mag[:, :nx]
            for o in range(zs):
                step = z - (o + 2)
                if -1 <= step <= 1:
                    for k in range(21):
                        term = fields[k] if step else 2.0 * fields[k]
                        boxes[o][k] = term if boxes[o][k] is None else boxes[o][k] + term
        for o in range(zs):
            for k in range(21):
                f = boxes[o][k]
                box = (pltpu.roll(f, 1, 1) + pltpu.roll(f, lanes - 1, 1) + 2.0 * f)[:, :nx] * 0.0625
                high = box.astype(jnp.bfloat16)
                cols = slice(o * nx, (o + 1) * nx)
                bhi[k, pl.ds(base, lp), cols] = high
                blo[k, pl.ds(base, lp), cols] = (box - high.astype(jnp.float32)).astype(jnp.bfloat16)

    @pl.loop(0, 21)
    def _(k):
        dot = functools.partial(jnp.dot, preferred_element_type=jnp.float32)
        filt[k] = dot(whi[...], bhi[k]) + (dot(whi[...], blo[k]) + dot(wlo[...], bhi[k]))

    @pl.loop(0, n)
    def _(p):
        base = pl.multiple_of(p * lp, 8)
        lm_total = jnp.zeros((lp, nx), jnp.float32)
        mm_total = jnp.zeros((lp, nx), jnp.float32)
        for o in range(zs):
            g = [filt[k, pl.ds(base, lp), o * nx : (o + 1) * nx] for k in range(21)]
            fmag = 4.0 * tensor_norm(g[3:9])
            for q, (i, j) in enumerate(PAIRS):
                leonard = g[9 + q] - g[i] * g[j]
                model = g[15 + q] - fmag * g[3 + q]
                weighted = model if q < 3 else 2.0 * model
                lm_total += leonard * weighted
                mm_total += model * weighted
                back[p, q, o] = leonard
        lms[pl.ds(base, lp), :] = lm_total
        mms[pl.ds(base, lp), :] = mm_total

    dot = functools.partial(jnp.dot, preferred_element_type=jnp.float32, precision=lax.Precision.HIGHEST)
    sums[0] = dot(onehot_t[...], lms[...])
    sums[1] = dot(onehot_t[...], mms[...])


def local(velocity, filter_inverse, filter_block, plane_bin):
    _, lp, nz, nx = velocity.shape
    n = lax.axis_size("pz")
    m = lax.axis_size("px")
    ny, zs = n * lp, nz // n
    win = zs + 4

    same = (filter_block[:, None] == filter_block[None, :]).astype(jnp.float32)
    masked = filter_inverse * same
    weights = masked / jnp.sum(masked, axis=1, keepdims=True)
    onehot = (plane_bin[:, None] == jnp.arange(NBIN, dtype=jnp.int32)[None, :]).astype(jnp.float32)

    turned = jnp.transpose(velocity, (0, 2, 1, 3))
    turned = jnp.concatenate([turned[:, -2:], turned, turned[:, :2]], axis=1)
    sent = jnp.stack([turned[:, t * zs : t * zs + win] for t in range(n)])
    own = lax.all_to_all(sent, "pz", split_axis=0, concat_axis=0, tiled=True)
    right = lax.ppermute(own, "px", [((i + 1) % m, i) for i in range(m)])
    left = right if m == 2 else lax.ppermute(own, "px", [(i, (i + 1) % m) for i in range(m)])

    back, sums = pl.pallas_call(
        functools.partial(column_kernel, (n, win, lp, nx)),
        out_shape=(
            jax.ShapeDtypeStruct((n, 7, zs, lp, nx), jnp.float32),
            jax.ShapeDtypeStruct((2, NBIN, nx), jnp.float32),
        ),
        in_specs=[pl.BlockSpec(memory_space=pltpu.VMEM)] * 5,
        out_specs=(pl.BlockSpec(memory_space=pltpu.VMEM),) * 2,
        scratch_shapes=[
            pltpu.VMEM((3, win, ny + 16, 2 * nx), jnp.float32),
            pltpu.VMEM((21, ny, zs * nx), jnp.bfloat16),
            pltpu.VMEM((21, ny, zs * nx), jnp.bfloat16),
            pltpu.VMEM((21, ny, zs * nx), jnp.float32),
            pltpu.VMEM((ny, nx), jnp.float32),
            pltpu.VMEM((ny, nx), jnp.float32),
            pltpu.VMEM((ny, ny), jnp.bfloat16),
            pltpu.VMEM((ny, ny), jnp.bfloat16),
        ],
        compiler_params=pltpu.CompilerParams(vmem_limit_bytes=60 * 1024 * 1024),
    )(own, right, left, weights, onehot.T)

    numer, denom = lax.psum(jnp.sum(sums, axis=2), ("px", "pz"))
    cells = nx * m * nz
    per_bin = numer / jnp.maximum(denom, jnp.float32(cells))
    coefficient = jnp.dot(onehot, per_bin, precision=lax.Precision.HIGHEST)

    home = lax.all_to_all(back, "pz", split_axis=0, concat_axis=0, tiled=True)
    home = jnp.transpose(home, (1, 3, 0, 2, 4)).reshape(7, lp, nz, nx)
    local_coef = lax.dynamic_slice_in_dim(coefficient, lax.axis_index("pz") * lp, lp, 0)
    viscosity = local_coef[:, None, None] * home[6]
    return (home[:6], viscosity, coefficient)


def solution(mesh):
    return jax.shard_map(
        local,
        mesh=mesh,
        in_specs=(P(None, "pz", None, "px"), P(), P(), P()),
        out_specs=(P(None, "pz", None, "px"), P("pz", None, "px"), P()),
        check_vma=False,
    )
```

time: 247 us -> 164 us (0.66)
  the two profiles are of different devices: /device:TPU:31 before, /device:TPU:0 now
where the time goes in v1:
time: 164 us; the launch traced here: 163 us
  blocking collectives  127 us (77%)
  Pallas kernels  20.6 us (13%)
  local copies, waits for them, and re-layouts  5.9 us (4%)
  starting transfers between devices  3.85 us (2%)
  other arithmetic  2.77 us (2%)
  waiting for transfers between devices  2.25 us (1%)
    psum x1, blocking collectives, local(): numer, denom = lax.psum(jnp.sum(sums, axis=2), ('px', 'pz'))  63.9 us
    all_to_all x1, blocking collectives, local(): own = lax.all_to_all(sent, 'pz', split_axis=0, concat_axis=0, tiled=True)  63.3 us
    pallas_call x1, Pallas kernels, local(): pl.pallas_call(functools.partial(column_kernel, (n, win, lp, nx)), out_sh...  20.6 us
    unnamed x30, local copies, waits for them, and re-layouts  5.43 us
    all_to_all x1, starting transfers between devices, local(): home = lax.all_to_all(back, 'pz', split_axis=0, concat_axis=0, tiled=True)  3.84 us
  transfers between devices with their start and end apart: 2, of which 1 were waited for; matrix products, arithmetic and copies ran while one was open for 1% of the time, Pallas kernels for 0%

profile of v1, /device:TPU:0, one launch (start us, length us, event | category | flops | bytes accessed | tf_op | source)
XLA Modules:
  0.0 163.5 jit_solution(16796389375397186860)
XLA Ops:
  0.6 1.6 copy.15
  2.6 0.0 copy-start.2
  2.6 0.0 copy-start.4
  2.6 0.0 copy-start.5
  2.6 63.3 %all_to_all.10.own = f32[16,3,6,16,128]{4,3,2,1,0:T(8,128)S(1)} all-to-all(f32[16,3,6,16,128]{4,3,2,1,0:T(8,128)S(1)} %fusion.3), channel_id=1, replica_groups=mesh['px'=2,'pz'=16] {'pz'}, dimensions={0} | all-to-all | bytes 4718592 | tf_op jit(solution)/shard_map/all_to_all | solution.py:129
  65.9 0.0 collective-permute-start
  65.9 0.2 fusion.1
  66.1 0.8 fusion.22.onehot_t
  66.9 0.4 copy-done.1
  67.3 0.8 fusion.weights
  68.2 2.3 %collective-permute-done.right.left = f32[16,3,6,16,128]{4,3,2,1,0:T(8,128)S(1)} collective-permute-done((f32[16,3,6,16,128]{4,3,2,1,0:T(8,128)S(1)}, f32[16,3,6,16,128]{4,3,2,1,0:T(8,128)S(1)}, u32[]{:S(2)}, u32[]{:S(2)}) %collective-permute-start) | collective-permute-done | bytes 2359328 | tf_op jit(solution)/shard_map/ppermute | solution.py:130
  70.4 1.4 copy-done
  71.8 20.6 %shard_map.67 = (f32[16,7,2,16,128]{4,3,2,1,0:T(8,128)}, f32[2,64,128]{2,1,0:T(8,128)}) custom-call(f32[16,3,6,16,128]{4,3,2,1,0:T(8,128)} %copy-done.1, f32[16,3,6,16,128]{4,3,2,1,0:T(8,128)} %copy-done, f32[16,3,6,16,128]{4,3,2,1,0:T(8,128)} %copy-done, f32[256,256]{1,0:T(8,128)} %fusion.weights, f32[64,256]{1,0:T(8,128)} %fusion.22.onehot_t), custom_call_target="tpu_custom_call" | custom-call | tf_op jit(solution)/shard_map/pallas_call | solution.py:133
  92.4 3.8 %all-to-all-start.1 = ((f32[16,7,2,16,128]{4,3,2,1,0:T(8,128)}), f32[16,7,2,16,128]{4,3,2,1,0:T(8,128)S(1)}, u32[]{:S(2)}, u32[]{:S(2)}) async-start(f32[16,7,2,16,128]{4,3,2,1,0:T(8,128)} %get-tuple-element.5), calls=%async_computation.1 | async-start | bytes 3670016 | tf_op jit(solution)/shard_map/all_to_all | solution.py:159
  96.2 0.1 reduce_sum.19
  96.3 63.9 %psum.7 = f32[2,64]{1,0:T(2,128)S(1)} all-reduce(f32[2,64]{1,0:T(2,128)S(1)} %reduce_sum.19), channel_id=1, replica_groups=mesh['px'=2,'pz'=16] {'px','pz'}, use_global_device_ids=true, to_apply=%region_2.0 | all-reduce | flops 128 | bytes 1024 | tf_op jit(solution)/shard_map/psum | solution.py:154
  160.2 0.2 fusion.20
  160.4 0.1 dynamic_slice.3
  160.5 0.0 all-to-all-done.1
  160.6 0.2 slice.103
  160.7 0.2 copy.10
  160.9 0.2 copy-done.6
  161.1 1.6 copy.12
  162.7 0.8 copy_multiply_fusion
  (26 shorter events, 0.2 us)
Async XLA Ops:
  2.6 63.3 %copy-start.2 = (f32[256,256]{1,0:T(8,128)S(1)}, f32[256,256]{1,0:T(8,128)}, u32[]{:S(2)}) copy-start(f32[256,256]{1,0:T(8,128)} %param.5) | copy-start | bytes 786436
  2.6 63.3 %copy-start.4 = (s32[256]{0:T(256)S(1)}, s32[256]{0:T(256)}, u32[]{:S(2)}) copy-start(s32[256]{0:T(256)} %param.6) | copy-start | bytes 3076
  2.6 63.5 %copy-start.5 = (s32[256]{0:T(256)S(1)}, s32[256]{0:T(256)}, u32[]{:S(2)}) copy-start(s32[256]{0:T(256)} %param.7) | copy-start | bytes 3076
  65.9 1.4 copy-start.1
  65.9 4.5 %collective-permute-start = (f32[16,3,6,16,128]{4,3,2,1,0:T(8,128)S(1)}, f32[16,3,6,16,128]{4,3,2,1,0:T(8,128)S(1)}, u32[]{:S(2)}, u32[]{:S(2)}) collective-permute-start(f32[16,3,6,16,128]{4,3,2,1,0:T(8,128)S(1)} %all_to_all.10.own), channel_id=1, source_target_pairs={{16,0},{0,16},{17,1},{1,17},{18,2},{2,18},{19,3},{3,19},{20,4},{4,... | collective-permute-start | bytes 7077896 | tf_op jit(solution)/shard_map/ppermute | solution.py:130
  70.4 1.4 copy-start
  92.4 3.9 %copy-start.3 = (f32[2,64,128]{2,1,0:T(8,128)S(1)}, f32[2,64,128]{2,1,0:T(8,128)}, u32[]{:S(2)}) copy-start(f32[2,64,128]{2,1,0:T(8,128)} %get-tuple-element.6) | copy-start | bytes 196612
  92.4 68.2 %all-to-all-start.1 = ((f32[16,7,2,16,128]{4,3,2,1,0:T(8,128)}), f32[16,7,2,16,128]{4,3,2,1,0:T(8,128)S(1)}, u32[]{:S(2)}, u32[]{:S(2)}) async-start(f32[16,7,2,16,128]{4,3,2,1,0:T(8,128)} %get-tuple-element.5), calls=%async_computation.1 | async-start | bytes 3670016 | tf_op jit(solution)/shard_map/all_to_all | solution.py:159
  160.4 0.7 copy-start.6

commit v2 on v1

v2 whole, which is shorter than its diff:
```python
import functools

import jax
import jax.numpy as jnp
from jax import lax
from jax.experimental import pallas as pl
from jax.experimental.pallas import tpu as pltpu
from jax.sharding import PartitionSpec as P

NBIN = 64
PAIRS = ((0, 0), (1, 1), (2, 2), (0, 1), (0, 2), (1, 2))


def tensor_norm(s):
    diag = s[0] * s[0] + s[1] * s[1] + s[2] * s[2]
    off = s[3] * s[3] + s[4] * s[4] + s[5] * s[5]
    return jnp.sqrt(2.0 * diag + 4.0 * off)


def strain_of(dx, dy, dz):
    return [
        dx[0] * 0.5,
        dy[1] * 0.5,
        dz[2] * 0.5,
        0.25 * (dy[0] + dx[1]),
        0.25 * (dz[0] + dx[2]),
        0.25 * (dz[1] + dy[2]),
    ]


def fill_from_blocks(dims, ext, own, right, left):
    n, win, lp, nx = dims
    lane = lax.broadcasted_iota(jnp.int32, (lp, nx), 1)
    from_right = lane < nx // 2

    @pl.loop(0, n)
    def _(p):
        rows = pl.ds(pl.multiple_of(8 + p * lp, 8), lp)
        for c in range(3):
            for z in range(win):
                ext[c, z, rows, 0:nx] = own[p, c, z]
                ext[c, z, rows, nx : 2 * nx] = jnp.where(from_right, right[p, c, z], left[p, c, z])


def fill_from_halves(dims, ext, core, own, other):
    n, win, lp, nx = dims
    half = win - 2
    here = core[0]
    main = 3 * half * lp

    def place(source, p, c, w, z):
        at = c * half + w
        rows = pl.ds(pl.multiple_of(8 + p * lp, 8), lp)
        ext[c, z, rows, 0:nx] = source[p, pl.ds(pl.multiple_of(at * lp, 8), lp), :]
        for r in range(lp // 8):
            shift = 2 * nx - 2 - 4 * (r * 3 * half + at)
            part = pltpu.roll(source[p, main : main + 8, :], lax.rem(shift, nx), 1)
            ext[c, z, pl.ds(pl.multiple_of(8 + p * lp + 8 * r, 8), 8), nx : 2 * nx] = part

    @pl.loop(0, n)
    def _(p):
        for c in range(3):
            for w in range(half):
                place(own, p, c, w, w + 2 * here)
            for w in range(2):
                place(other, p, c, w + (half - 2) * here, w + half * (1 - here))


def column_kernel(dims, fill, sources, *refs):
    n, win, lp, nx = dims
    blocks, refs = refs[:sources], refs[sources:]
    weights, onehot, back, ext, bhi, blo, filt, lms, mms, whi, wlo = refs
    zs = win - 4
    ny = n * lp
    lanes = 2 * nx
    heavy = weights[...].astype(jnp.bfloat16)
    whi[...] = heavy
    wlo[...] = (weights[...] - heavy.astype(jnp.float32)).astype(jnp.bfloat16)

    zero = jnp.zeros((8, lanes), jnp.float32)
    for c in range(3):
        for z in range(win):
            ext[c, z, 0:8, :] = zero
            ext[c, z, ny + 8 : ny + 16, :] = zero
    fill(dims, ext, *blocks)

    @pl.loop(0, n)
    def _(p):
        base = pl.multiple_of(p * lp, 8)
        u = [[ext[c, z, pl.ds(base + 8, lp), :] for z in range(win)] for c in range(3)]
        boxes = [[None] * 21 for _ in range(zs)]
        for z in range(1, win - 1):
            v = [u[c][z] for c in range(3)]
            dx, dy, dz = [], [], []
            for c in range(3):
                dx.append(pltpu.roll(v[c], lanes - 1, 1) - pltpu.roll(v[c], 1, 1))
                tall = ext[c, z, pl.ds(base, lp + 16), :]
                dy.append(tall[9 : 9 + lp] - tall[7 : 7 + lp])
                dz.append(u[c][z + 1] - u[c][z - 1])
            s = strain_of(dx, dy, dz)
            mag = tensor_norm(s)
            fields = v + s + [v[i] * v[j] for i, j in PAIRS] + [mag * t for t in s]
            for o in range(zs):
                step = z - (o + 2)
                if -1 <= step <= 1:
                    for k in range(21):
                        term = fields[k] if step else 2.0 * fields[k]
                        boxes[o][k] = term if boxes[o][k] is None else boxes[o][k] + term
        for o in range(zs):
            for k in range(21):
                f = boxes[o][k]
                box = (pltpu.roll(f, 1, 1) + pltpu.roll(f, lanes - 1, 1) + 2.0 * f)[:, :nx] * 0.0625
                high = box.astype(jnp.bfloat16)
                cols = slice(o * nx, (o + 1) * nx)
                bhi[k, pl.ds(base, lp), cols] = high
                blo[k, pl.ds(base, lp), cols] = (box - high.astype(jnp.float32)).astype(jnp.bfloat16)

    @pl.loop(0, 21)
    def _(k):
        dot = functools.partial(jnp.dot, preferred_element_type=jnp.float32)
        filt[k] = dot(whi[...], bhi[k]) + (dot(whi[...], blo[k]) + dot(wlo[...], bhi[k]))

    @pl.loop(0, n)
    def _(p):
        base = pl.multiple_of(p * lp, 8)
        lm_total = jnp.zeros((lp, nx), jnp.float32)
        mm_total = jnp.zeros((lp, nx), jnp.float32)
        for o in range(zs):
            g = [filt[k, pl.ds(base, lp), o * nx : (o + 1) * nx] for k in range(21)]
            fmag = 4.0 * tensor_norm(g[3:9])
            for q, (i, j) in enumerate(PAIRS):
                leonard = g[9 + q] - g[i] * g[j]
                model = g[15 + q] - fmag * g[3 + q]
                weighted = model if q < 3 else 2.0 * model
                lm_total += leonard * weighted
                mm_total += model * weighted
                back[p, (q * zs + o) * lp : (q * zs + o + 1) * lp, :] = leonard
        lms[pl.ds(base, lp), :] = lm_total
        mms[pl.ds(base, lp), :] = mm_total

    ones = jnp.ones((8, nx), jnp.float32)
    exact = functools.partial(
        lax.dot_general, preferred_element_type=jnp.float32, precision=lax.Precision.HIGHEST
    )
    totals = []
    for part in (lms, mms):
        planes = exact(ones, part[...], (((1,), (1,)), ((), ())))
        totals.append(exact(planes, onehot[...], (((1,), (0,)), ((), ()))))
    row = lax.broadcasted_iota(jnp.int32, (8, onehot.shape[1]), 0)
    tile = jnp.where(row < 4, totals[0], totals[1])
    for p in range(n):
        back[p, 6 * zs * lp :, :] = tile


def magnitude_kernel(centre, right, left, below, above, out):
    _, lp, nz, nx = centre.shape
    lane = lax.broadcasted_iota(jnp.int32, (nz, nx), 1)
    for y in range(lp):
        v = [centre[c, y] for c in range(3)]
        dx, dy, dz = [], [], []
        for c in range(3):
            ahead = jnp.where(lane == nx - 1, pltpu.roll(right[c, y], nx - 1, 1), pltpu.roll(v[c], nx - 1, 1))
            behind = jnp.where(lane == 0, pltpu.roll(left[c, y], 1, 1), pltpu.roll(v[c], 1, 1))
            dx.append(ahead - behind)
            dz.append(pltpu.roll(v[c], nz - 1, 0) - pltpu.roll(v[c], 1, 0))
            up = centre[c, y + 1] if y + 1 < lp else above[c, 0]
            down = centre[c, y - 1] if y else below[c, 0]
            dy.append(up - down)
        out[y] = tensor_norm(strain_of(dx, dy, dz))


def local(velocity, filter_inverse, filter_block, plane_bin):
    _, lp, nz, nx = velocity.shape
    n = lax.axis_size("pz")
    m = lax.axis_size("px")
    ny, zs = n * lp, nz // n
    win = zs + 4
    half = zs + 2
    shared = m == 2 and n % 2 == 0 and 12 * half * (lp // 8) <= nx
    swap = [(0, 1), (1, 0)]
    core = lax.axis_index("px")

    same = (filter_block[:, None] == filter_block[None, :]).astype(jnp.float32)
    masked = filter_inverse * same
    weights = masked / jnp.sum(masked, axis=1, keepdims=True)
    onehot = (plane_bin[:, None] == jnp.arange(nx, dtype=jnp.int32)[None, :]).astype(jnp.float32)

    right = lax.ppermute(velocity, "px", [((i + 1) % m, i) for i in range(m)])
    left = right if m == 2 else lax.ppermute(velocity, "px", [(i, (i + 1) % m) for i in range(m)])
    below = lax.ppermute(velocity[:, -1:], "pz", [(i, i + 1) for i in range(n - 1)])
    above = lax.ppermute(velocity[:, :1], "pz", [(i + 1, i) for i in range(n - 1)])
    magnitude = pl.pallas_call(
        magnitude_kernel,
        out_shape=jax.ShapeDtypeStruct((lp, nz, nx), jnp.float32),
        cost_estimate=pl.CostEstimate(flops=60 * lp * nz * nx, bytes_accessed=40 * lp * nz * nx, transcendentals=0),
    )(velocity, right, left, below, above)

    if shared:
        zg = 2 * zs
        chunks, edges = [], []
        halves = [jnp.where(core == h, velocity, right) for h in range(2)]
        for h in range(2):
            outer = halves[1 - h]
            edge = jnp.concatenate([outer[..., -2:], outer[..., :2]], axis=3)
            for part, dest in ((halves[h], chunks), (edge, edges)):
                turned = jnp.transpose(part, (0, 2, 1, 3))
                turned = jnp.concatenate([turned[:, -2:], turned, turned[:, :2]], axis=1)
                turned = lax.dynamic_slice_in_dim(turned, core * half, nz - zg + half, 1)
                dest.append(jnp.stack([turned[:, g * zg : g * zg + half] for g in range(n // 2)]))
        main = jnp.stack(chunks, axis=1).reshape(n, 3 * half * lp, nx)
        edge = jnp.stack(edges, axis=1).reshape(n, 3, half, lp // 8, 8, 4)
        edge = jnp.transpose(edge, (0, 4, 3, 1, 2, 5)).reshape(n, 8, 12 * half * (lp // 8))
        edge = jnp.pad(edge, ((0, 0), (0, 0), (0, nx - edge.shape[2])))
        sent = jnp.concatenate([main, edge], axis=1)
        own = lax.all_to_all(sent, "pz", split_axis=0, concat_axis=0, tiled=True)
        other = lax.ppermute(own, "px", swap)
        fill, blocks = fill_from_halves, (core.astype(jnp.int32).reshape(1), own, other)
        specs = [pl.BlockSpec(memory_space=pltpu.SMEM)] + [pl.BlockSpec(memory_space=pltpu.VMEM)] * 2
    else:
        turned = jnp.transpose(velocity, (0, 2, 1, 3))
        turned = jnp.concatenate([turned[:, -2:], turned, turned[:, :2]], axis=1)
        sent = jnp.stack([turned[:, t * zs : t * zs + win] for t in range(n)])
        own = lax.all_to_all(sent, "pz", split_axis=0, concat_axis=0, tiled=True)
        ahead = lax.ppermute(own, "px", [((i + 1) % m, i) for i in range(m)])
        behind = lax.ppermute(own, "px", [(i, (i + 1) % m) for i in range(m)])
        fill, blocks = fill_from_blocks, (own, ahead, behind)
        specs = [pl.BlockSpec(memory_space=pltpu.VMEM)] * 3

    rows = 6 * zs * lp
    back = pl.pallas_call(
        functools.partial(column_kernel, (n, win, lp, nx), fill, len(blocks)),
        out_shape=jax.ShapeDtypeStruct((n, rows + 8, nx), jnp.float32),
        in_specs=specs + [pl.BlockSpec(memory_space=pltpu.VMEM)] * 2,
        out_specs=pl.BlockSpec(memory_space=pltpu.VMEM),
        scratch_shapes=[
            pltpu.VMEM((3, win, ny + 16, 2 * nx), jnp.float32),
            pltpu.VMEM((21, ny, zs * nx), jnp.bfloat16),
            pltpu.VMEM((21, ny, zs * nx), jnp.bfloat16),
            pltpu.VMEM((21, ny, zs * nx), jnp.float32),
            pltpu.VMEM((ny, nx), jnp.float32),
            pltpu.VMEM((ny, nx), jnp.float32),
            pltpu.VMEM((ny, ny), jnp.bfloat16),
            pltpu.VMEM((ny, ny), jnp.bfloat16),
        ],
        compiler_params=pltpu.CompilerParams(vmem_limit_bytes=60 * 1024 * 1024),
    )(*blocks, weights, onehot)

    home = lax.all_to_all(back, "pz", split_axis=0, concat_axis=0, tiled=True)
    totals = jnp.sum(home[:, rows:], axis=0)
    stress = home[:, :rows]
    if shared:
        totals = totals + lax.ppermute(totals, "px", swap)
        stress = stress.reshape(n // 2, 2, 6, zs, lp, nx)
        mine = lax.dynamic_index_in_dim(stress, core, 1, keepdims=False)
        give = lax.dynamic_index_in_dim(stress, 1 - core, 1, keepdims=False)
        got = lax.ppermute(give, "px", swap)
        first, second = jnp.where(core == 0, mine, got), jnp.where(core == 0, got, mine)
        stress = jnp.stack([first, second], axis=1)
        leonard = jnp.transpose(stress, (2, 4, 0, 1, 3, 5)).reshape(6, lp, nz, nx)
    else:
        totals = lax.psum(totals, "px")
        stress = stress.reshape(n, 6, zs, lp, nx)
        leonard = jnp.transpose(stress, (1, 3, 0, 2, 4)).reshape(6, lp, nz, nx)
    numer, denom = totals[0, :NBIN], totals[4, :NBIN]
    cells = nx * m * nz
    per_bin = numer / jnp.maximum(denom, jnp.float32(cells))
    coefficient = jnp.dot(onehot[:, :NBIN], per_bin, precision=lax.Precision.HIGHEST)
    local_coef = lax.dynamic_slice_in_dim(coefficient, lax.axis_index("pz") * lp, lp, 0)
    viscosity = local_coef[:, None, None] * magnitude
    return (leonard, viscosity, coefficient)


def solution(mesh):
    return jax.shard_map(
        local,
        mesh=mesh,
        in_specs=(P(None, "pz", None, "px"), P(), P(), P()),
        out_specs=(P(None, "pz", None, "px"), P("pz", None, "px"), P()),
        check_vma=False,
    )
```

time: 164 us -> 157 us (0.957)
  the two profiles are of different devices: /device:TPU:0 before, /device:TPU:16 now
where the time goes in v2:
time: 157 us
  waiting for transfers between devices  48.6 us (31%)
  blocking collectives  44.9 us (29%)
  Pallas kernels  24.7 us (16%)
  local copies, waits for them, and re-layouts  16.7 us (11%)
  starting transfers between devices  12.1 us (8%)
  other arithmetic  8.68 us (6%)
    all_to_all x1, blocking collectives, local(): own = lax.all_to_all(sent, 'pz', split_axis=0, concat_axis=0, tiled=True)  44.9 us
    all_to_all x1, waiting for transfers between devices, local(): home = lax.all_to_all(back, 'pz', split_axis=0, concat_axis=0, tiled=True)  39.1 us
    pallas_call x1, Pallas kernels, local(): pl.pallas_call(functools.partial(column_kernel, (n, win, lp, nx), fill, l...  21.5 us
    all_to_all x1, starting transfers between devices, local(): home = lax.all_to_all(back, 'pz', split_axis=0, concat_axis=0, tiled=True)  5.96 us
    ppermute x1, waiting for transfers between devices, local(): lax.ppermute(velocity[:, -1:], 'pz', [(i, i + 1) for i in range(n - 1)])  5.54 us
    slice x6, local copies, waits for them, and re-layouts, local(): edge = jnp.concatenate([outer[..., -2:], outer[..., :2]], axis=3)  5.37 us
    unnamed x33, local copies, waits for them, and re-layouts  4 us
    ppermute x1, starting transfers between devices, local(): lax.ppermute(velocity[:, :1], 'pz', [(i + 1, i) for i in range(n - 1)])  3.82 us
  transfers between devices with their start and end apart: 7, of which 4 were waited for; matrix products, arithmetic and copies ran while one was open for 3% of the time, Pallas kernels for 2%

profile of v2, /device:TPU:16, one launch (start us, length us, event | category | flops | bytes accessed | tf_op | source)
XLA Modules:
  0.0 156.8 jit_solution(7901950417121069507)
XLA Ops:
  0.7 2.5 %collective-permute-done.right.left = f32[3,16,32,128]{3,2,1,0:T(8,128)S(1)} collective-permute-done((f32[3,16,32,128]{3,2,1,0:T(8,128)}, f32[3,16,32,128]{3,2,1,0:T(8,128)S(1)}, u32[]{:S(2)}, u32[]{:S(2)}) %collective-permute-start) | collective-permute-done | bytes 786464 | tf_op jit(solution)/shard_map/ppermute | solution.py:188
  3.2 1.6 %broadcast_select_fusion = (f32[3,16,32,128]{3,2,1,0:T(8,128)S(1)}, f32[3,16,32,128]{3,2,1,0:T(8,128)S(1)}) fusion(f32[3,16,32,128]{3,2,1,0:T(8,128)} %centre.1, f32[3,16,32,128]{3,2,1,0:T(8,128)S(1)} %collective-permute-done.right.left, pred[]{:T(512)S(6)} %eq.17, pred[]{:T(512)S(6)} %eq.16), kind=kLoop, calls=%fused_computation.20 | loop fusion | flops 393216 | bytes 3145730 | tf_op jit(solution)/shard_map/jit(_where)/select_n | solution.py:201
  5.1 1.4 fusion.35
  6.6 0.7 fusion.1
  7.9 0.7 pad_maximum_fusion
  8.8 1.5 copy.23
  10.3 1.5 copy.24
  17.9 44.9 %all_to_all.10.refs_1_ = f32[16,200,128]{2,1,0:T(8,128)S(1)} all-to-all(f32[16,200,128]{2,1,0:T(8,128)S(1)} %select_maximum_fusion), channel_id=1, replica_groups=mesh['px'=2,'pz'=16] {'pz'}, dimensions={0} | all-to-all | bytes 3276800 | tf_op jit(solution)/shard_map/all_to_all | solution.py:215
  63.0 1.0 iota_compare_fusion.1
  64.0 0.8 fusion.6.refs_3_
  64.9 1.5 collective-permute-done.1.refs_2_
  66.3 1.2 copy-done.2
  67.5 21.5 %shard_map.67 = f32[16,200,128]{2,1,0:T(8,128)} custom-call(s32[1]{0:T(128)} %bitcast.refs_0_, f32[16,200,128]{2,1,0:T(8,128)} %copy-done.1, f32[16,200,128]{2,1,0:T(8,128)} %copy-done.2, f32[256,256]{1,0:T(8,128)} %fusion.6.refs_3_, f32[256,128]{1,0:T(8,128)} %get-tuple-element.44.refs_4_), custom_call_target="tpu_custom_call" | custom-call | tf_op jit(solution)/shard_map/pallas_call | solution.py:230
  89.0 6.0 %all-to-all-start.1 = ((f32[16,200,128]{2,1,0:T(8,128)}), f32[16,200,128]{2,1,0:T(8,128)S(1)}, u32[]{:S(2)}, u32[]{:S(2)}) async-start(f32[16,200,128]{2,1,0:T(8,128)} %shard_map.67), calls=%async_computation.1 | async-start | bytes 3276800 | tf_op jit(solution)/shard_map/all_to_all | solution.py:248
  95.0 39.1 %all-to-all-done.1 = f32[16,200,128]{2,1,0:T(8,128)S(1)} async-done(((f32[16,200,128]{2,1,0:T(8,128)}), f32[16,200,128]{2,1,0:T(8,128)S(1)}, u32[]{:S(2)}, u32[]{:S(2)}) %all-to-all-start.1) | async-done | bytes 1638432 | tf_op jit(solution)/shard_map/all_to_all | solution.py:248
  134.2 1.0 dynamic-slice_bitcast_fusion
  135.2 0.8 fusion.32
  136.0 3.8 %collective-permute-start.5 = (f32[3,1,32,128]{3,2,1,0:T(8,128)S(1)}, f32[3,1,32,128]{3,2,1,0:T(8,128)S(1)}, u32[]{:S(2)}, u32[]{:S(2)}) collective-permute-start(f32[3,1,32,128]{3,2,1,0:T(8,128)S(1)} %get-tuple-element.13), channel_id=1, source_target_pairs={{1,0},{2,1},{3,2},{4,3},{5,4},{6,5},{7,6},{8,7},{9,8},{10,9},{11,1... | collective-permute-start | bytes 147464 | tf_op jit(solution)/shard_map/ppermute | solution.py:191
  139.8 2.0 %collective-permute-start.4 = (f32[3,1,32,128]{3,2,1,0:T(8,128)S(1)}, f32[3,1,32,128]{3,2,1,0:T(8,128)S(1)}, u32[]{:S(2)}, u32[]{:S(2)}) collective-permute-start(f32[3,1,32,128]{3,2,1,0:T(8,128)S(1)} %get-tuple-element.14), channel_id=1, source_target_pairs={{0,1},{1,2},{2,3},{3,4},{4,5},{5,6},{6,7},{7,8},{8,9},{9,10},{10,1... | collective-permute-start | bytes 147464 | tf_op jit(solution)/shard_map/ppermute | solution.py:190
  142.1 5.5 %collective-permute-done.4.below = f32[3,1,32,128]{3,2,1,0:T(8,128)S(1)} collective-permute-done((f32[3,1,32,128]{3,2,1,0:T(8,128)S(1)}, f32[3,1,32,128]{3,2,1,0:T(8,128)S(1)}, u32[]{:S(2)}, u32[]{:S(2)}) %collective-permute-start.4) | collective-permute-done | bytes 49184 | tf_op jit(solution)/shard_map/ppermute | solution.py:190
  148.2 3.2 %shard_map.68 = f32[16,32,128]{2,1,0:T(8,128)} custom-call(f32[3,16,32,128]{3,2,1,0:T(8,128)} %centre.1, f32[3,16,32,128]{3,2,1,0:T(8,128)} %copy-done, f32[3,16,32,128]{3,2,1,0:T(8,128)} %copy-done, f32[3,1,32,128]{3,2,1,0:T(8,128)} %copy-done.5, f32[3,1,32,128]{3,2,1,0:T(8,128)} %copy-done.4), custom_call_target="tpu_custom_call" | custom-call | flops 3932160 | bytes 2621440 | tf_op jit(solution)/shard_map/pallas_call | solution.py:192
  151.7 1.7 %broadcast_multiply_fusion = f32[16,32,128]{2,1,0:T(8,128)} fusion(f32[16,32,128]{2,1,0:T(8,128)} %shard_map.68, f32[16]{0:T(128)S(1)} %dynamic_slice.28), kind=kLoop, calls=%fused_computation.25 | loop fusion | flops 65536 | bytes 524352 | tf_op jit(solution)/shard_map/mul | solution.py:269
  153.5 1.3 fusion.4
  155.2 1.6 %copy.49 = f32[6,16,32,128]{3,2,1,0:T(8,128)} copy(f32[6,16,32,128]{3,1,2,0:T(8,128)S(1)} %bitcast.145) | data formatting | bytes 3145728
  (85 shorter events, 9.0 us)
Async XLA Ops:
  0.6 2.6 %collective-permute-start = (f32[3,16,32,128]{3,2,1,0:T(8,128)}, f32[3,16,32,128]{3,2,1,0:T(8,128)S(1)}, u32[]{:S(2)}, u32[]{:S(2)}) collective-permute-start(f32[3,16,32,128]{3,2,1,0:T(8,128)} %centre.1), channel_id=1, source_target_pairs={{16,0},{0,16},{17,1},{1,17},{18,2},{2,18},{19,3},{3,19},{20,4},{4,... | collective-permute-start | bytes 2359304 | tf_op jit(solution)/shard_map/ppermute | solution.py:188
  3.2 1.6 %copy-start = (f32[3,16,32,128]{3,2,1,0:T(8,128)}, f32[3,16,32,128]{3,2,1,0:T(8,128)S(1)}, u32[]{:S(2)}) copy-start(f32[3,16,32,128]{3,2,1,0:T(8,128)S(1)} %collective-permute-done.right.left) | copy-start | bytes 2359300
  17.9 45.0 %copy-start.3 = (f32[256,256]{1,0:T(8,128)S(1)}, f32[256,256]{1,0:T(8,128)}, u32[]{:S(2)}) copy-start(f32[256,256]{1,0:T(8,128)} %param.5) | copy-start | bytes 786436
  17.9 45.0 %copy-start.6 = (s32[256]{0:T(256)S(1)}, s32[256]{0:T(256)}, u32[]{:S(2)}) copy-start(s32[256]{0:T(256)} %param.6) | copy-start | bytes 3076
  17.9 45.2 %copy-start.7 = (s32[256]{0:T(256)S(1)}, s32[256]{0:T(256)}, u32[]{:S(2)}) copy-start(s32[256]{0:T(256)} %param.7) | copy-start | bytes 3076
  62.8 3.5 %copy-start.1 = (f32[16,200,128]{2,1,0:T(8,128)}, f32[16,200,128]{2,1,0:T(8,128)S(1)}, u32[]{:S(2)}) copy-start(f32[16,200,128]{2,1,0:T(8,128)S(1)} %all_to_all.10.refs_1_) | copy-start | bytes 4915204
  62.8 3.5 %collective-permute-start.1 = (f32[16,200,128]{2,1,0:T(8,128)S(1)}, f32[16,200,128]{2,1,0:T(8,128)S(1)}, u32[]{:S(2)}, u32[]{:S(2)}) collective-permute-start(f32[16,200,128]{2,1,0:T(8,128)S(1)} %all_to_all.10.refs_1_), channel_id=1, source_target_pairs={{0,16},{16,0},{1,17},{17,1},{2,18},{18,2},{3,19},{19,3},{4,20},{20... | collective-permute-start | bytes 4915208 | tf_op jit(solution)/shard_map/ppermute | solution.py:216
  66.3 1.2 copy-start.2
  89.0 45.0 %all-to-all-start.1 = ((f32[16,200,128]{2,1,0:T(8,128)}), f32[16,200,128]{2,1,0:T(8,128)S(1)}, u32[]{:S(2)}, u32[]{:S(2)}) async-start(f32[16,200,128]{2,1,0:T(8,128)} %shard_map.67), calls=%async_computation.1 | async-start | bytes 3276800 | tf_op jit(solution)/shard_map/all_to_all | solution.py:248
  135.2 18.3 %collective-permute-start.2 = (f32[8,6,2,16,128]{4,3,2,1,0:T(8,128)}, f32[8,6,2,16,128]{4,3,2,1,0:T(8,128)}, u32[]{:S(2)}, u32[]{:S(2)}) collective-permute-start(f32[8,6,2,16,128]{4,3,2,1,0:T(8,128)} %dynamic-slice_bitcast_fusion), channel_id=1, source_target_pairs={{0,16},{16,0},{1,17},{17,1},{2,18},{18,2},{3,19},{19,3},{4,20},{20... | collective-permute-start | bytes 2359304 | tf_op jit(solution)/shard_map/ppermute | solution.py:256
  136.0 6.1 %collective-permute-start.5 = (f32[3,1,32,128]{3,2,1,0:T(8,128)S(1)}, f32[3,1,32,128]{3,2,1,0:T(8,128)S(1)}, u32[]{:S(2)}, u32[]{:S(2)}) collective-permute-start(f32[3,1,32,128]{3,2,1,0:T(8,128)S(1)} %get-tuple-element.13), channel_id=1, source_target_pairs={{1,0},{2,1},{3,2},{4,3},{5,4},{6,5},{7,6},{8,7},{9,8},{10,9},{11,1... | collective-permute-start | bytes 147464 | tf_op jit(solution)/shard_map/ppermute | solution.py:191
  139.8 7.8 %collective-permute-start.4 = (f32[3,1,32,128]{3,2,1,0:T(8,128)S(1)}, f32[3,1,32,128]{3,2,1,0:T(8,128)S(1)}, u32[]{:S(2)}, u32[]{:S(2)}) collective-permute-start(f32[3,1,32,128]{3,2,1,0:T(8,128)S(1)} %get-tuple-element.14), channel_id=1, source_target_pairs={{0,1},{1,2},{2,3},{3,4},{4,5},{5,6},{6,7},{7,8},{8,9},{9,10},{10,1... | collective-permute-start | bytes 147464 | tf_op jit(solution)/shard_map/ppermute | solution.py:190
  141.9 9.6 %collective-permute-start.3 = (f32[8,128]{1,0:T(8,128)S(1)}, f32[8,128]{1,0:T(8,128)S(1)}, u32[]{:S(2)}, u32[]{:S(2)}) collective-permute-start(f32[8,128]{1,0:T(8,128)S(1)} %slice_reduce_fusion), channel_id=1, source_target_pairs={{0,16},{16,0},{1,17},{17,1},{2,18},{18,2},{3,19},{19,3},{4,20},{20... | collective-permute-start | bytes 12296 | tf_op jit(solution)/shard_map/ppermute | solution.py:252
  142.1 5.5 %copy-start.4 = (f32[3,1,32,128]{3,2,1,0:T(8,128)}, f32[3,1,32,128]{3,2,1,0:T(8,128)S(1)}, u32[]{:S(2)}) copy-start(f32[3,1,32,128]{3,2,1,0:T(8,128)S(1)} %collective-permute-done.5.above) | copy-start | bytes 147460
  147.6 0.6 copy-start.5
  151.6 3.2 %copy-start.8 = (f32[1,256]{1,0:T(1,128)}, f32[1,256]{1,0:T(1,128)S(1)}, u32[]{:S(2)}) copy-start(f32[1,256]{1,0:T(1,128)S(1)} %fusion.8) | copy-start | bytes 3076

commit v3 on v2

--- a/solution.py
+++ b/solution.py
@@ -8,6 +8,7 @@
 from jax.sharding import PartitionSpec as P
 
 NBIN = 64
+MESH = pl.DeviceIdType.MESH
 PAIRS = ((0, 0), (1, 1), (2, 2), (0, 1), (0, 2), (1, 2))
 
 
@@ -46,12 +47,10 @@
     n, win, lp, nx = dims
     half = win - 2
     here = core[0]
-    main = 3 * half * lp
-
-    def place(source, p, c, w, z):
-        at = c * half + w
+
+    def place(source, main, p, c, w, at, z):
         rows = pl.ds(pl.multiple_of(8 + p * lp, 8), lp)
-        ext[c, z, rows, 0:nx] = source[p, pl.ds(pl.multiple_of(at * lp, 8), lp), :]
+        ext[c, z, rows, 0:nx] = source[p, (w * 3 + c) * lp : (w * 3 + c + 1) * lp, :]
         for r in range(lp // 8):
             shift = 2 * nx - 2 - 4 * (r * 3 * half + at)
             part = pltpu.roll(source[p, main : main + 8, :], lax.rem(shift, nx), 1)
@@ -61,9 +60,10 @@
     def _(p):
         for c in range(3):
             for w in range(half):
-                place(own, p, c, w, w + 2 * here)
+                place(own, 3 * half * lp, p, c, w, w * 3 + c, w + 2 * here)
             for w in range(2):
-                place(other, p, c, w + (half - 2) * here, w + half * (1 - here))
+                at = (w + (half - 2) * here) * 3 + c
+                place(other, 6 * lp, p, c, w, at, w + half * (1 - here))
 
 
 def column_kernel(dims, fill, sources, *refs):
@@ -152,6 +152,135 @@
         back[p, 6 * zs * lp :, :] = tile
 
 
+def greet_all(m, n):
+    me = lax.axis_index("px") * n + lax.axis_index("pz")
+    barrier = pltpu.get_barrier_semaphore()
+
+    @pl.loop(1, m * n)
+    def _(step):
+        peer = lax.rem(me + step, m * n)
+        pl.semaphore_signal(barrier, inc=1, device_id=(peer // n, lax.rem(peer, n)), device_id_type=MESH)
+
+    pl.semaphore_wait(barrier, m * n - 1)
+
+
+def outward_kernel(dims, main, edge, own, other, main_out, main_in, edge_out, edge_in, pass_out, pass_in):
+    n, half, lp = dims
+    a, s = lax.axis_index("px"), lax.axis_index("pz")
+    rows = 3 * half * lp
+    greet_all(2, n)
+
+    def send(source, t, parity, dst, out_sem, in_sem):
+        core, chip = lax.rem(t, 2), 2 * (t // 2) + parity
+        itself = (core == a) & (chip == s)
+        copy = pltpu.make_async_remote_copy(
+            source.at[t], dst, out_sem.at[t], in_sem.at[s], device_id=(core, chip), device_id_type=MESH
+        )
+        return itself, copy, pltpu.make_async_copy(source.at[t], dst, in_sem.at[s])
+
+    def sends(t):
+        return (
+            send(edge, t, 1 - a, own.at[s, rows : rows + 8], edge_out, edge_in),
+            send(main, t, a, own.at[s, 0:rows], main_out, main_in),
+        )
+
+    @pl.loop(0, n)
+    def _(i):
+        for itself, copy, here in sends(lax.rem(s + i, n)):
+            pl.when(itself)(here.start)
+            pl.when(jnp.logical_not(itself))(copy.start)
+
+    first = (1 - a) * (half - 2) * 3 * lp
+
+    def passes(p):
+        return [
+            pltpu.make_async_remote_copy(
+                own.at[p, src], other.at[p, dst], pass_out.at[j, p], pass_in.at[j, p],
+                device_id=(1 - a, s), device_id_type=MESH,
+            )
+            for j, (src, dst) in enumerate(
+                (
+                    (pl.ds(pl.multiple_of(first, 8), 6 * lp), slice(0, 6 * lp)),
+                    (slice(rows, rows + 8), slice(6 * lp, 6 * lp + 8)),
+                )
+            )
+        ]
+
+    @pl.loop(0, n)
+    def _(i):
+        p = lax.rem(s + n - i, n)
+        pltpu.make_async_copy(main.at[0], own.at[p, 0:rows], main_in.at[p]).wait()
+        pltpu.make_async_copy(edge.at[0], own.at[p, rows : rows + 8], edge_in.at[p]).wait()
+        for copy in passes(p):
+            copy.start()
+
+    @pl.loop(0, n)
+    def _(p):
+        for copy in passes(p):
+            copy.wait()
+        for itself, copy, here in sends(p):
+            pl.when(jnp.logical_not(itself))(copy.wait_send)
+
+
+def return_kernel(n, back, velocity, home, out, beside, near, back_out, back_in, halo_out, halo_in):
+    _, lp, nz, nx = velocity.shape
+    a, s = lax.axis_index("px"), lax.axis_index("pz")
+    greet_all(2, n)
+    slot = 2 * (s // 2) + a
+    parity = lax.rem(s, 2)
+    remote = functools.partial(pltpu.make_async_remote_copy, device_id_type=MESH)
+    halos = [
+        remote(velocity, beside, halo_out.at[0], halo_in.at[0], device_id=(1 - a, s)),
+        remote(velocity.at[:, lp - 1], near.at[0], halo_out.at[1], halo_in.at[1], device_id=(a, lax.rem(s + 1, n))),
+        remote(velocity.at[:, 0], near.at[1], halo_out.at[2], halo_in.at[2], device_id=(a, lax.rem(s + n - 1, n))),
+    ]
+    for copy in halos:
+        copy.start()
+
+    def send(p):
+        itself = (parity == a) & (p == s)
+        copy = remote(back.at[p], home.at[slot], back_out.at[p], back_in.at[slot], device_id=(parity, p))
+        return itself, copy, pltpu.make_async_copy(back.at[p], home.at[slot], back_in.at[slot])
+
+    @pl.loop(0, n)
+    def _(i):
+        itself, copy, here = send(lax.rem(s + i, n))
+        pl.when(itself)(here.start)
+        pl.when(jnp.logical_not(itself))(copy.start)
+
+    for copy in halos:
+        copy.wait()
+    lane = lax.broadcasted_iota(jnp.int32, (nz, nx), 1)
+    has_below = (s > 0).astype(jnp.float32)
+    has_above = (s < n - 1).astype(jnp.float32)
+
+    def plane(y, ups, downs):
+        dx, dy, dz = [], [], []
+        for c in range(3):
+            v, side = velocity[c, y], beside[c, y]
+            ahead = jnp.where(lane == nx - 1, pltpu.roll(side, nx - 1, 1), pltpu.roll(v, nx - 1, 1))
+            behind = jnp.where(lane == 0, pltpu.roll(side, 1, 1), pltpu.roll(v, 1, 1))
+            dx.append(ahead - behind)
+            dz.append(pltpu.roll(v, nz - 1, 0) - pltpu.roll(v, 1, 0))
+            dy.append(ups[c] - downs[c])
+        out[y] = tensor_norm(strain_of(dx, dy, dz))
+
+    line = [near[0, c] * has_below for c in range(3)]
+    plane(0, [velocity[c, 1] for c in range(3)], line)
+    line = [near[1, c] * has_above for c in range(3)]
+    plane(lp - 1, line, [velocity[c, lp - 2] for c in range(3)])
+
+    @pl.loop(1, lp - 1)
+    def _(y):
+        plane(y, [velocity[c, y + 1] for c in range(3)], [velocity[c, y - 1] for c in range(3)])
+
+    @pl.loop(0, n)
+    def _(p):
+        pltpu.make_async_copy(back.at[0], home.at[p], back_in.at[p]).wait()
+        itself, copy, here = send(p)
+        pl.when(jnp.logical_not(itself))(copy.wait_send)
+
+
 def magnitude_kernel(centre, right, left, below, above, out):
     _, lp, nz, nx = centre.shape
     lane = lax.broadcasted_iota(jnp.int32, (nz, nx), 1)
@@ -177,7 +306,6 @@
     win = zs + 4
     half = zs + 2
     shared = m == 2 and n % 2 == 0 and 12 * half * (lp // 8) <= nx
-    swap = [(0, 1), (1, 0)]
     core = lax.axis_index("px")
 
     same = (filter_block[:, None] == filter_block[None, :]).astype(jnp.float32)
@@ -185,38 +313,41 @@
     weights = masked / jnp.sum(masked, axis=1, keepdims=True)
     onehot = (plane_bin[:, None] == jnp.arange(nx, dtype=jnp.int32)[None, :]).astype(jnp.float32)
 
-    right = lax.ppermute(velocity, "px", [((i + 1) % m, i) for i in range(m)])
-    left = right if m == 2 else lax.ppermute(velocity, "px", [(i, (i + 1) % m) for i in range(m)])
-    below = lax.ppermute(velocity[:, -1:], "pz", [(i, i + 1) for i in range(n - 1)])
-    above = lax.ppermute(velocity[:, :1], "pz", [(i + 1, i) for i in range(n - 1)])
-    magnitude = pl.pallas_call(
-        magnitude_kernel,
-        out_shape=jax.ShapeDtypeStruct((lp, nz, nx), jnp.float32),
-        cost_estimate=pl.CostEstimate(flops=60 * lp * nz * nx, bytes_accessed=40 * lp * nz * nx, transcendentals=0),
-    )(velocity, right, left, below, above)
-
     if shared:
         zg = 2 * zs
-        chunks, edges = [], []
-        halves = [jnp.where(core == h, velocity, right) for h in range(2)]
-        for h in range(2):
-            outer = halves[1 - h]
-            edge = jnp.concatenate([outer[..., -2:], outer[..., :2]], axis=3)
-            for part, dest in ((halves[h], chunks), (edge, edges)):
-                turned = jnp.transpose(part, (0, 2, 1, 3))
-                turned = jnp.concatenate([turned[:, -2:], turned, turned[:, :2]], axis=1)
-                turned = lax.dynamic_slice_in_dim(turned, core * half, nz - zg + half, 1)
-                dest.append(jnp.stack([turned[:, g * zg : g * zg + half] for g in range(n // 2)]))
-        main = jnp.stack(chunks, axis=1).reshape(n, 3 * half * lp, nx)
-        edge = jnp.stack(edges, axis=1).reshape(n, 3, half, lp // 8, 8, 4)
-        edge = jnp.transpose(edge, (0, 4, 3, 1, 2, 5)).reshape(n, 8, 12 * half * (lp // 8))
+        chunks = []
+        for part in (velocity, jnp.concatenate([velocity[..., -2:], velocity[..., :2]], axis=3)):
+            turned = jnp.transpose(part, (2, 0, 1, 3))
+            turned = jnp.concatenate([turned[-2:], turned, turned[:2]], axis=0)
+            starts = [(t // 2) * zg + (t % 2) * half for t in range(n)]
+            chunks.append(jnp.stack([turned[i : i + half] for i in starts]))
+        main = chunks[0].reshape(n, 3 * half * lp, nx)
+        edge = chunks[1].reshape(n, half * 3, lp // 8, 8, 4)
+        edge = jnp.transpose(edge, (0, 3, 2, 1, 4)).reshape(n, 8, 12 * half * (lp // 8))
         edge = jnp.pad(edge, ((0, 0), (0, 0), (0, nx - edge.shape[2])))
-        sent = jnp.concatenate([main, edge], axis=1)
-        own = lax.all_to_all(sent, "pz", split_axis=0, concat_axis=0, tiled=True)
-        other = lax.ppermute(own, "px", swap)
+        own, other = pl.pallas_call(
+            functools.partial(outward_kernel, (n, half, lp)),
+            out_shape=(
+                jax.ShapeDtypeStruct((n, 3 * half * lp + 8, nx), jnp.float32),
+                jax.ShapeDtypeStruct((n, 6 * lp + 8, nx), jnp.float32),
+            ),
+            in_specs=[pl.BlockSpec(memory_space=pltpu.VMEM)] * 2,
+            out_specs=(pl.BlockSpec(memory_space=pltpu.VMEM),) * 2,
+            scratch_shapes=[pltpu.SemaphoreType.DMA((n,))] * 4 + [pltpu.SemaphoreType.DMA((2, n))] * 2,
+            compiler_params=pltpu.CompilerParams(collective_id=0, has_side_effects=True),
+        )(main, edge)
         fill, blocks = fill_from_halves, (core.astype(jnp.int32).reshape(1), own, other)
         specs = [pl.BlockSpec(memory_space=pltpu.SMEM)] + [pl.BlockSpec(memory_space=pltpu.VMEM)] * 2
     else:
+        right = lax.ppermute(velocity, "px", [((i + 1) % m, i) for i in range(m)])
+        left = right if m == 2 else lax.ppermute(velocity, "px", [(i, (i + 1) % m) for i in range(m)])
+        below = lax.ppermute(velocity[:, -1:], "pz", [(i, i + 1) for i in range(n - 1)])
+        above = lax.ppermute(velocity[:, :1], "pz", [(i + 1, i) for i in range(n - 1)])
+        magnitude = pl.pallas_call(
+            magnitude_kernel,
+            out_shape=jax.ShapeDtypeStruct((lp, nz, nx), jnp.float32),
+            cost_estimate=pl.CostEstimate(flops=60 * lp * nz * nx, bytes_accessed=40 * lp * nz * nx, transcendentals=0),
+        )(velocity, right, left, below, above)
         turned = jnp.transpose(velocity, (0, 2, 1, 3))
         turned = jnp.concatenate([turned[:, -2:], turned, turned[:, :2]], axis=1)
         sent = jnp.stack([turned[:, t * zs : t * zs + win] for t in range(n)])
@@ -245,22 +376,32 @@
         compiler_params=pltpu.CompilerParams(vmem_limit_bytes=60 * 1024 * 1024),
     )(*blocks, weights, onehot)
 
-    home = lax.all_to_all(back, "pz", split_axis=0, concat_axis=0, tiled=True)
-    totals = jnp.sum(home[:, rows:], axis=0)
-    stress = home[:, :rows]
     if shared:
-        totals = totals + lax.ppermute(totals, "px", swap)
-        stress = stress.reshape(n // 2, 2, 6, zs, lp, nx)
-        mine = lax.dynamic_index_in_dim(stress, core, 1, keepdims=False)
-        give = lax.dynamic_index_in_dim(stress, 1 - core, 1, keepdims=False)
-        got = lax.ppermute(give, "px", swap)
-        first, second = jnp.where(core == 0, mine, got), jnp.where(core == 0, got, mine)
-        stress = jnp.stack([first, second], axis=1)
-        leonard = jnp.transpose(stress, (2, 4, 0, 1, 3, 5)).reshape(6, lp, nz, nx)
+        home, magnitude = pl.pallas_call(
+            functools.partial(return_kernel, n),
+            out_shape=(
+                jax.ShapeDtypeStruct(back.shape, jnp.float32),
+                jax.ShapeDtypeStruct((lp, nz, nx), jnp.float32),
+            ),
+            in_specs=[pl.BlockSpec(memory_space=pltpu.VMEM)] * 2,
+            out_specs=(pl.BlockSpec(memory_space=pltpu.VMEM),) * 2,
+            scratch_shapes=[
+                pltpu.VMEM((3, lp, nz, nx), jnp.float32),
+                pltpu.VMEM((2, 3, nz, nx), jnp.float32),
+                pltpu.SemaphoreType.DMA((n,)),
+                pltpu.SemaphoreType.DMA((n,)),
+                pltpu.SemaphoreType.DMA((3,)),
+                pltpu.SemaphoreType.DMA((3,)),
+            ],
+            compiler_params=pltpu.CompilerParams(collective_id=1, has_side_effects=True),
+        )(back, velocity)
+        totals = jnp.sum(home[:, rows:], axis=0)
+        totals = totals + lax.ppermute(totals, "px", [(0, 1), (1, 0)])
     else:
-        totals = lax.psum(totals, "px")
-        stress = stress.reshape(n, 6, zs, lp, nx)
-        leonard = jnp.transpose(stress, (1, 3, 0, 2, 4)).reshape(6, lp, nz, nx)
+        home = lax.all_to_all(back, "pz", split_axis=0, concat_axis=0, tiled=True)
+        totals = lax.psum(jnp.sum(home[:, rows:], axis=0), "px")
+    stress = home[:, :rows].reshape(n, 6, zs, lp, nx)
+    leonard = jnp.transpose(stress, (1, 3, 0, 2, 4)).reshape(6, lp, nz, nx)
     numer, denom = totals[0, :NBIN], totals[4, :NBIN]
     cells = nx * m * nz
     per_bin = numer / jnp.maximum(denom, jnp.float32(cells))

time: 157 us -> 141 us (0.90)
  the two profiles are of different devices: /device:TPU:16 before, /device:TPU:31 now
where the time goes in v3:
time: 141 us; the launch traced here: 140 us
  Pallas kernels  114 us (81%)
  local copies, waits for them, and re-layouts  20.5 us (15%)
  other arithmetic  4.02 us (3%)
    pallas_call x1, Pallas kernels, local(): pl.pallas_call(functools.partial(return_kernel, n), out_shape=(jax.ShapeD...  47.4 us
    pallas_call x1, Pallas kernels, local(): pl.pallas_call(functools.partial(outward_kernel, (n, half, lp)), out_shap...  45.3 us
    pallas_call x1, Pallas kernels, local(): pl.pallas_call(functools.partial(column_kernel, (n, win, lp, nx), fill, l...  21.3 us
    unnamed x44, local copies, waits for them, and re-layouts  10.6 us
  transfers between devices with their start and end apart: 1, of which 0 were waited for; matrix products, arithmetic and copies ran while one was open for 3% of the time, Pallas kernels for 0%

profile of v3, /device:TPU:31, one launch (start us, length us, event | category | flops | bytes accessed | tf_op | source)
XLA Modules:
  0.0 140.5 jit_solution(17268398986336617915)
XLA Ops:
  0.7 1.9 %fusion.10 = (f32[3,16,32,2]{3,2,1,0:T(8,128)S(1)}, f32[3,16,32,2]{3,2,1,0:T(8,128)S(1)}) fusion(f32[3,16,32,128]{3,2,1,0:T(8,128)} %velocity.1), kind=kLoop, calls=%fused_computation.52 | loop fusion | bytes 49152 | tf_op jit(solution)/shard_map/slice | solution.py:319
  2.6 0.7 iota_compare_fusion
  3.6 0.8 fusion.refs_3_
  4.8 0.6 constant_dynamic-update-slice_fusion.15
  5.5 0.6 constant_dynamic-update-slice_fusion.14
  6.1 0.6 constant_dynamic-update-slice_fusion.13
  6.8 0.6 constant_dynamic-update-slice_fusion.12
  7.4 0.6 constant_dynamic-update-slice_fusion.11
  8.1 0.6 constant_dynamic-update-slice_fusion.10
  8.7 0.6 constant_dynamic-update-slice_fusion.9
  9.4 0.6 constant_dynamic-update-slice_fusion.8
  10.0 0.6 constant_dynamic-update-slice_fusion.7
  10.6 0.6 constant_dynamic-update-slice_fusion.6
  11.3 0.6 constant_dynamic-update-slice_fusion.5
  13.2 0.6 constant_dynamic-update-slice_fusion.2
  18.9 0.7 constant_dynamic-update-slice_fusion.main
  20.2 45.3 %shard_map.67 = (f32[16,200,128]{2,1,0:T(8,128)}, f32[16,104,128]{2,1,0:T(8,128)}) custom-call(f32[16,192,128]{2,1,0:T(8,128)} %constant_dynamic-update-slice_fusion.main, f32[16,8,128]{2,1,0:T(8,128)} %pad.4.edge), custom_call_target="tpu_custom_call" | custom-call | tf_op jit(solution)/shard_map/pallas_call | solution.py:328
  65.5 21.3 %shard_map.68.back = f32[16,200,128]{2,1,0:T(8,128)} custom-call(s32[1]{0:T(128)} %bitcast.refs_0_, f32[16,200,128]{2,1,0:T(8,128)} %get-tuple-element.7.refs_1_, f32[16,104,128]{2,1,0:T(8,128)} %get-tuple-element.8.refs_2_, f32[256,256]{1,0:T(8,128)} %fusion.refs_3_, f32[256,128]{1,0:T(8,128)} %get-tuple-element.36.refs_4_), custom_call_target="tpu_custom_call" | custom-call | tf_op jit(solution)/shard_map/pallas_call | solution.py:361
  86.8 47.4 %shard_map.69 = (f32[16,200,128]{2,1,0:T(8,128)}, f32[16,32,128]{2,1,0:T(8,128)}) custom-call(f32[16,200,128]{2,1,0:T(8,128)} %shard_map.68.back, f32[3,16,32,128]{3,2,1,0:T(8,128)} %velocity.1), custom_call_target="tpu_custom_call" | custom-call | tf_op jit(solution)/shard_map/pallas_call | solution.py:380
  134.3 0.9 slice_reduce_fusion
  135.1 0.7 collective-permute-start
  135.8 1.5 %slice.129 = f32[16,192,128]{2,1,0:T(8,128)S(1)} slice(f32[16,200,128]{2,1,0:T(8,128)} %get-tuple-element.9), slice={[0:16], [0:192], [0:128]} | slice | bytes 3145728 | tf_op jit(solution)/shard_map/slice | solution.py:403
  137.4 2.0 %copy.60 = f32[6,16,16,2,128]{4,3,2,1,0:T(2,128)} copy(f32[6,16,16,2,128]{4,1,3,0,2:T(8,128)S(1)} %bitcast.44) | data formatting | bytes 3145728 | tf_op jit(solution)/shard_map/transpose | solution.py:404
  139.7 0.8 broadcast_multiply_fusion
  (73 shorter events, 7.6 us)
Async XLA Ops:
  0.6 1.9 %copy-start = (f32[3,16,32,128]{3,2,1,0:T(8,128)S(1)}, f32[3,16,32,128]{3,2,1,0:T(8,128)}, u32[]{:S(2)}) copy-start(f32[3,16,32,128]{3,2,1,0:T(8,128)} %velocity.1) | copy-start | bytes 2359300
  0.6 2.0 %copy-start.4 = (s32[256]{0:T(256)S(1)}, s32[256]{0:T(256)}, u32[]{:S(2)}) copy-start(s32[256]{0:T(256)} %param.7) | copy-start | bytes 3076
  0.7 2.7 %copy-start.1 = (f32[256,256]{1,0:T(8,128)S(1)}, f32[256,256]{1,0:T(8,128)}, u32[]{:S(2)}) copy-start(f32[256,256]{1,0:T(8,128)} %param.5) | copy-start | bytes 786436
  0.7 2.7 %copy-start.3 = (s32[256]{0:T(256)S(1)}, s32[256]{0:T(256)}, u32[]{:S(2)}) copy-start(s32[256]{0:T(256)} %param.6) | copy-start | bytes 3076
  135.1 4.3 %collective-permute-start = (f32[8,128]{1,0:T(8,128)S(1)}, f32[8,128]{1,0:T(8,128)S(1)}, u32[]{:S(2)}, u32[]{:S(2)}) collective-permute-start(f32[8,128]{1,0:T(8,128)S(1)} %slice_reduce_fusion), channel_id=1, source_target_pairs={{0,16},{16,0},{1,17},{17,1},{2,18},{18,2},{3,19},{19,3},{4,20},{20... | collective-permute-start | bytes 12296 | tf_op jit(solution)/shard_map/ppermute | solution.py:399
  137.4 2.3 %copy-start.2 = (f32[16,32,128]{2,1,0:T(8,128)S(1)}, f32[16,32,128]{2,1,0:T(8,128)}, u32[]{:S(2)}) copy-start(f32[16,32,128]{2,1,0:T(8,128)} %get-tuple-element.10) | copy-start | bytes 786436
  139.5 0.9 copy-start.5

commit v4 on v3

--- a/solution.py
+++ b/solution.py
@@ -43,27 +43,27 @@
                 ext[c, z, rows, nx : 2 * nx] = jnp.where(from_right, right[p, c, z], left[p, c, z])
 
 
-def fill_from_halves(dims, ext, core, own, other):
+def fill_from_halves(dims, ext, core, own, own_edge, other, other_edge):
     n, win, lp, nx = dims
     half = win - 2
     here = core[0]
 
-    def place(source, main, p, c, w, at, z):
+    def place(source, edges, p, c, w, at, z):
         rows = pl.ds(pl.multiple_of(8 + p * lp, 8), lp)
-        ext[c, z, rows, 0:nx] = source[p, (w * 3 + c) * lp : (w * 3 + c + 1) * lp, :]
+        ext[c, z, rows, 0:nx] = source[p, w, c * lp : (c + 1) * lp, :]
         for r in range(lp // 8):
             shift = 2 * nx - 2 - 4 * (r * 3 * half + at)
-            part = pltpu.roll(source[p, main : main + 8, :], lax.rem(shift, nx), 1)
+            part = pltpu.roll(edges[p], lax.rem(shift, nx), 1)
             ext[c, z, pl.ds(pl.multiple_of(8 + p * lp + 8 * r, 8), 8), nx : 2 * nx] = part
 
     @pl.loop(0, n)
     def _(p):
         for c in range(3):
             for w in range(half):
-                place(own, 3 * half * lp, p, c, w, w * 3 + c, w + 2 * here)
+                place(own, own_edge, p, c, w, w * 3 + c, w + 2 * here)
             for w in range(2):
                 at = (w + (half - 2) * here) * 3 + c
-                place(other, 6 * lp, p, c, w, at, w + half * (1 - here))
+                place(other, other_edge, p, c, w, at, w + half * (1 - here))
 
 
 def column_kernel(dims, fill, sources, *refs):
@@ -164,24 +164,39 @@
     pl.semaphore_wait(barrier, m * n - 1)
 
 
-def outward_kernel(dims, main, edge, own, other, main_out, main_in, edge_out, edge_in, pass_out, pass_in):
+def edge_kernel(dims, main, edge):
+    half, lp, nx = dims
+    lane = lax.broadcasted_iota(jnp.int32, (8, nx), 1)
+
+    @pl.loop(0, edge.shape[0])
+    def _(i):
+        tile = jnp.zeros((8, nx), jnp.float32)
+        for r in range(lp // 8):
+            for w in range(half):
+                for c in range(3):
+                    at = 4 * ((r * half + w) * 3 + c)
+                    cells = main[i * half + w, c * lp + r * 8 : c * lp + r * 8 + 8, :]
+                    tile = jnp.where((lane >= at) & (lane < at + 4), pltpu.roll(cells, (at + 2) % nx, 1), tile)
+        edge[i] = tile
+
+
+def outward_kernel(dims, main, edge, own, own_edge, other, other_edge, main_out, main_in, edge_out, edge_in, pass_out, pass_in):
     n, half, lp = dims
     a, s = lax.axis_index("px"), lax.axis_index("pz")
-    rows = 3 * half * lp
     greet_all(2, n)
 
     def send(source, t, parity, dst, out_sem, in_sem):
         core, chip = lax.rem(t, 2), 2 * (t // 2) + parity
         itself = (core == a) & (chip == s)
         copy = pltpu.make_async_remote_copy(
-            source.at[t], dst, out_sem.at[t], in_sem.at[s], device_id=(core, chip), device_id_type=MESH
+            source, dst, out_sem.at[t], in_sem.at[s], device_id=(core, chip), device_id_type=MESH
         )
-        return itself, copy, pltpu.make_async_copy(source.at[t], dst, in_sem.at[s])
+        return itself, copy, pltpu.make_async_copy(source, dst, in_sem.at[s])
 
     def sends(t):
         return (
-            send(edge, t, 1 - a, own.at[s, rows : rows + 8], edge_out, edge_in),
-            send(main, t, a, own.at[s, 0:rows], main_out, main_in),
+            send(edge.at[t // 2 + lax.rem(t, 2)], t, 1 - a, own_edge.at[s], edge_out, edge_in),
+            send(main.at[pl.ds((t // 2 + lax.rem(t, 2)) * half, half)], t, a, own.at[s], main_out, main_in),
         )
 
     @pl.loop(0, n)
@@ -190,27 +205,24 @@
             pl.when(itself)(here.start)
             pl.when(jnp.logical_not(itself))(copy.start)
 
-    first = (1 - a) * (half - 2) * 3 * lp
+    first = (1 - a) * (half - 2)
 
     def passes(p):
         return [
             pltpu.make_async_remote_copy(
-                own.at[p, src], other.at[p, dst], pass_out.at[j, p], pass_in.at[j, p],
+                src, dst, pass_out.at[j, p], pass_in.at[j, p],
                 device_id=(1 - a, s), device_id_type=MESH,
             )
             for j, (src, dst) in enumerate(
-                (
-                    (pl.ds(pl.multiple_of(first, 8), 6 * lp), slice(0, 6 * lp)),
-                    (slice(rows, rows + 8), slice(6 * lp, 6 * lp + 8)),
-                )
+                ((own.at[p, pl.ds(first, 2)], other.at[p]), (own_edge.at[p], other_edge.at[p]))
             )
         ]
 
     @pl.loop(0, n)
     def _(i):
         p = lax.rem(s + n - i, n)
-        pltpu.make_async_copy(main.at[0], own.at[p, 0:rows], main_in.at[p]).wait()
-        pltpu.make_async_copy(edge.at[0], own.at[p, rows : rows + 8], edge_in.at[p]).wait()
+        pltpu.make_async_copy(main.at[0:half], own.at[p], main_in.at[p]).wait()
+        pltpu.make_async_copy(edge.at[0], own_edge.at[p], edge_in.at[p]).wait()
         for copy in passes(p):
             copy.start()
 
@@ -305,7 +317,7 @@
     ny, zs = n * lp, nz // n
     win = zs + 4
     half = zs + 2
-    shared = m == 2 and n % 2 == 0 and 12 * half * (lp // 8) <= nx
+    shared = m == 2 and n % 2 == 0 and n > 2 and half == 2 * zs and 12 * half * (lp // 8) <= nx
     core = lax.axis_index("px")
 
     same = (filter_block[:, None] == filter_block[None, :]).astype(jnp.float32)
@@ -314,30 +326,27 @@
     onehot = (plane_bin[:, None] == jnp.arange(nx, dtype=jnp.int32)[None, :]).astype(jnp.float32)
 
     if shared:
-        zg = 2 * zs
-        chunks = []
-        for part in (velocity, jnp.concatenate([velocity[..., -2:], velocity[..., :2]], axis=3)):
-            turned = jnp.transpose(part, (2, 0, 1, 3))
-            turned = jnp.concatenate([turned[-2:], turned, turned[:2]], axis=0)
-            starts = [(t // 2) * zg + (t % 2) * half for t in range(n)]
-            chunks.append(jnp.stack([turned[i : i + half] for i in starts]))
-        main = chunks[0].reshape(n, 3 * half * lp, nx)
-        edge = chunks[1].reshape(n, half * 3, lp // 8, 8, 4)
-        edge = jnp.transpose(edge, (0, 3, 2, 1, 4)).reshape(n, 8, 12 * half * (lp // 8))
-        edge = jnp.pad(edge, ((0, 0), (0, 0), (0, nx - edge.shape[2])))
-        own, other = pl.pallas_call(
+        turned = jnp.transpose(velocity, (2, 0, 1, 3)).reshape(nz, 3 * lp, nx)
+        main = jnp.concatenate([turned[-2:], turned, turned[:2]], axis=0)
+        edge = pl.pallas_call(
+            functools.partial(edge_kernel, (half, lp, nx)),
+            out_shape=jax.ShapeDtypeStruct((n // 2 + 1, 8, nx), jnp.float32),
+        )(main)
+        own, own_edge, other, other_edge = pl.pallas_call(
             functools.partial(outward_kernel, (n, half, lp)),
             out_shape=(
-                jax.ShapeDtypeStruct((n, 3 * half * lp + 8, nx), jnp.float32),
-                jax.ShapeDtypeStruct((n, 6 * lp + 8, nx), jnp.float32),
+                jax.ShapeDtypeStruct((n, half, 3 * lp, nx), jnp.float32),
+                jax.ShapeDtypeStruct((n, 8, nx), jnp.float32),
+                jax.ShapeDtypeStruct((n, 2, 3 * lp, nx), jnp.float32),
+                jax.ShapeDtypeStruct((n, 8, nx), jnp.float32),
             ),
             in_specs=[pl.BlockSpec(memory_space=pltpu.VMEM)] * 2,
-            out_specs=(pl.BlockSpec(memory_space=pltpu.VMEM),) * 2,
+            out_specs=(pl.BlockSpec(memory_space=pltpu.VMEM),) * 4,
             scratch_shapes=[pltpu.SemaphoreType.DMA((n,))] * 4 + [pltpu.SemaphoreType.DMA((2, n))] * 2,
             compiler_params=pltpu.CompilerParams(collective_id=0, has_side_effects=True),
         )(main, edge)
-        fill, blocks = fill_from_halves, (core.astype(jnp.int32).reshape(1), own, other)
-        specs = [pl.BlockSpec(memory_space=pltpu.SMEM)] + [pl.BlockSpec(memory_space=pltpu.VMEM)] * 2
+        fill, blocks = fill_from_halves, (core.astype(jnp.int32).reshape(1), own, own_edge, other, other_edge)
+        specs = [pl.BlockSpec(memory_space=pltpu.SMEM)] + [pl.BlockSpec(memory_space=pltpu.VMEM)] * 4
     else:
         right = lax.ppermute(velocity, "px", [((i + 1) % m, i) for i in range(m)])
         left = right if m == 2 else lax.ppermute(velocity, "px", [(i, (i + 1) % m) for i in range(m)])

time: 141 us -> 129 us (0.915)
  local copies, waits for them, and re-layouts: 20.5 us -> 6.41 us
  Pallas kernels: 114 us -> 117 us
    unnamed x44 -> x10, local copies, waits for them, and re-layouts: 10.6 us -> 0.02 us
    pallas_call x0 -> x1, Pallas kernels: none -> 2.64 us  [local(): pl.pallas_call(functools.partial(edge_kernel, (half, lp, nx)), out_shape=...]
    slice x21 -> x3, local copies, waits for them, and re-layouts: 3.28 us -> 1.12 us  [local(): main = jnp.concatenate([turned[-2:], turned, turned[:2]], axis=0)]
    another operation x11 -> x0, local copies, waits for them, and re-layouts: 1.71 us -> none  [local(): chunks.append(jnp.stack([turned[i:i + half] for i in starts]))]
where the time goes in v4:
time: 129 us
  Pallas kernels  117 us (91%)
  local copies, waits for them, and re-layouts  6.41 us (5%)
  other arithmetic  4.41 us (3%)
    pallas_call x1, Pallas kernels, local(): pl.pallas_call(functools.partial(return_kernel, n), out_shape=(jax.ShapeD...  47.5 us
    pallas_call x1, Pallas kernels, local(): pl.pallas_call(functools.partial(outward_kernel, (n, half, lp)), out_shap...  45.1 us
    pallas_call x1, Pallas kernels, local(): pl.pallas_call(functools.partial(column_kernel, (n, win, lp, nx), fill, l...  21.3 us
    pallas_call x1, Pallas kernels, local(): pl.pallas_call(functools.partial(edge_kernel, (half, lp, nx)), out_shape=...  2.64 us
  transfers between devices with their start and end apart: 1, of which 0 were waited for; matrix products, arithmetic and copies ran while one was open for 3% of the time, Pallas kernels for 0%

profile of v4, /device:TPU:31, one launch (start us, length us, event | category | flops | bytes accessed | tf_op | source)
XLA Modules:
  0.0 128.9 jit_solution(11919600758105364836)
XLA Ops:
  0.6 0.0 copy-start.3
  0.6 0.0 copy-start.2
  0.7 0.0 copy-start
  0.7 1.1 fusion.10
  1.8 1.6 %copy.8 = f32[32,3,16,128]{3,2,1,0:T(8,128)S(1)} copy(f32[32,3,16,128]{3,0,2,1:T(8,128)} %bitcast.16) | data formatting | bytes 1572864 | tf_op jit(solution)/shard_map/transpose | solution.py:329
  3.4 0.0 copy-done.3
  3.4 0.8 iota_compare_fusion
  4.2 0.0 copy-done.2
  4.2 0.2 fusion.1
  4.4 0.8 fusion.refs_5_
  5.2 1.0 pad_maximum_fusion.main
  6.2 2.6 %shard_map.67.edge = f32[9,8,128]{2,1,0:T(8,128)} custom-call(f32[36,48,128]{2,1,0:T(8,128)} %pad_maximum_fusion.main), custom_call_target="tpu_custom_call" | custom-call | tf_op jit(solution)/shard_map/pallas_call | solution.py:331
  8.8 45.1 %shard_map.68 = (f32[16,4,48,128]{3,2,1,0:T(8,128)}, f32[16,8,128]{2,1,0:T(8,128)}, f32[16,2,48,128]{3,2,1,0:T(8,128)}, f32[16,8,128]{2,1,0:T(8,128)}) custom-call(f32[36,48,128]{2,1,0:T(8,128)} %pad_maximum_fusion.main, f32[9,8,128]{2,1,0:T(8,128)} %shard_map.67.edge), custom_call_target="tpu_custom_call" | custom-call | tf_op jit(solution)/shard_map/pallas_call | solution.py:335
  53.9 21.3 %shard_map.69.back = f32[16,200,128]{2,1,0:T(8,128)} custom-call(s32[1]{0:T(128)} %bitcast.refs_0_, f32[16,4,48,128]{3,2,1,0:T(8,128)} %get-tuple-element.9.refs_1_, f32[16,8,128]{2,1,0:T(8,128)} %get-tuple-element.10.refs_2_, f32[16,2,48,128]{3,2,1,0:T(8,128)} %get-tuple-element.11.refs_3_, f32[16,8,128]{2,1,0:T(8,128)} %get-tuple-element.12.refs_4_, ...), custom_call_target="tpu_custom_call" | custom-call | tf_op jit(solution)/shard_map/pallas_call | solution.py:370
  75.2 47.5 %shard_map.70 = (f32[16,200,128]{2,1,0:T(8,128)}, f32[16,32,128]{2,1,0:T(8,128)}) custom-call(f32[16,200,128]{2,1,0:T(8,128)} %shard_map.69.back, f32[3,16,32,128]{3,2,1,0:T(8,128)} %velocity.1), custom_call_target="tpu_custom_call" | custom-call | tf_op jit(solution)/shard_map/pallas_call | solution.py:389
  122.7 0.9 slice_reduce_fusion
  123.6 0.7 collective-permute-start
  124.3 1.5 %slice.31 = f32[16,192,128]{2,1,0:T(8,128)S(1)} slice(f32[16,200,128]{2,1,0:T(8,128)} %get-tuple-element.13), slice={[0:16], [0:192], [0:128]} | slice | bytes 3145728 | tf_op jit(solution)/shard_map/slice | solution.py:412
  125.8 2.0 %copy.10 = f32[6,16,16,2,128]{4,3,2,1,0:T(2,128)} copy(f32[6,16,16,2,128]{4,1,3,0,2:T(8,128)S(1)} %bitcast.14) | data formatting | bytes 3145728 | tf_op jit(solution)/shard_map/transpose | solution.py:413
  127.8 0.0 collective-permute-done
  127.8 0.1 fusion.2
  128.0 0.1 dynamic_slice.3
  128.1 0.0 copy-done.1
  128.1 0.8 broadcast_multiply_fusion
  (7 shorter events, 0.0 us)
Async XLA Ops:
  0.6 2.8 %copy-start.3 = (s32[256]{0:T(256)S(1)}, s32[256]{0:T(256)}, u32[]{:S(2)}) copy-start(s32[256]{0:T(256)} %param.7) | copy-start | bytes 3076
  0.6 3.5 %copy-start.2 = (s32[256]{0:T(256)S(1)}, s32[256]{0:T(256)}, u32[]{:S(2)}) copy-start(s32[256]{0:T(256)} %param.6) | copy-start | bytes 3076
  0.7 3.5 %copy-start = (f32[256,256]{1,0:T(8,128)S(1)}, f32[256,256]{1,0:T(8,128)}, u32[]{:S(2)}) copy-start(f32[256,256]{1,0:T(8,128)} %param.5) | copy-start | bytes 786436
  123.6 4.3 %collective-permute-start = (f32[8,128]{1,0:T(8,128)S(1)}, f32[8,128]{1,0:T(8,128)S(1)}, u32[]{:S(2)}, u32[]{:S(2)}) collective-permute-start(f32[8,128]{1,0:T(8,128)S(1)} %slice_reduce_fusion), channel_id=1, source_target_pairs={{0,16},{16,0},{1,17},{17,1},{2,18},{18,2},{3,19},{19,3},{4,20},{20... | collective-permute-start | bytes 12296 | tf_op jit(solution)/shard_map/ppermute | solution.py:408
  125.8 2.3 %copy-start.1 = (f32[16,32,128]{2,1,0:T(8,128)S(1)}, f32[16,32,128]{2,1,0:T(8,128)}, u32[]{:S(2)}) copy-start(f32[16,32,128]{2,1,0:T(8,128)} %get-tuple-element.14) | copy-start | bytes 786436
  128.0 0.9 copy-start.4
